TPU v7x, 32 devices: a whole 2x2x4 slice. The times are simulated.
32 devices in a mesh: dp: 8 (over z, y), mp: 4 (over x, core).
Axes of the slice: x: 2, y: 2, z: 4, core: 2. Of those that a mesh axis runs over, the one named last changes fastest.
Arguments:
- tokens: bfloat16 [16384, 768], P(('dp', 'mp')), may hold values from -6 to 6
- segment_lengths: int32 [32, 8], P('dp'), may hold values from 1 to 192, 512 in all within a row
- gain_one: float32 [768], replicated, may hold values from 0.5 to 1.5
- shift_one: float32 [768], replicated, may hold values from -1.25 to 1.25
- qkv_weight: bfloat16 [3, 768, 768], P(None, None, 'mp'), may hold values from -0.21875 to 0.21875
- qv_bias: float32 [2, 768], P(None, 'mp'), may hold values from -1.75 to 1.75
- out_weight: bfloat16 [768, 768], P('mp'), may hold values from -1.25 to 1.25
- out_bias: float32 [768], replicated, may hold values from -1.25 to 1.25
- gain_two: float32 [768], replicated, may hold values from 0.5 to 1.5
- shift_two: float32 [768], replicated, may hold values from -1.25 to 1.25
- up_weight: bfloat16 [768, 3072], P(None, 'mp'), may hold values from -0.21875 to 0.21875
- up_bias: float32 [3072], P('mp'), may hold values from -1.75 to 1.75
- down_weight: bfloat16 [3072, 768], P('mp'), may hold values from -0.109375 to 0.109375
- down_bias: float32 [768], replicated, may hold values from -1.25 to 1.25
- cotangent: bfloat16 [16384, 768], P(('dp', 'mp')), may hold values from -8 to 8
Outputs:
- layer_output: float32 [16384, 768], P(('dp', 'mp'))
- token_grad: float32 [16384, 768], P(('dp', 'mp'))
- gain_one_grad: float32 [768], replicated
- shift_one_grad: float32 [768], replicated
- qkv_weight_grad: float32 [3, 768, 768], P(None, None, 'mp')
- qv_bias_grad: float32 [2, 768], P(None, 'mp')
- out_weight_grad: float32 [768, 768], P('mp')
- out_bias_grad: float32 [768], replicated
- gain_two_grad: float32 [768], replicated
- shift_two_grad: float32 [768], replicated
- up_weight_grad: float32 [768, 3072], P(None, 'mp')
- up_bias_grad: float32 [3072], P('mp')
- down_weight_grad: float32 [3072, 768], P('mp')
- down_bias_grad: float32 [768], replicated
Inputs may be any that keep to these rules, and one draw needn't show every extreme that they name: `segment_lengths`: each row sums to 512; its largest entry is 192.
All inputs are finite; a program needn't handle non-finite values.
Results may differ from a plain program's by a relative error of at most 0.014.
Values may be sent and summed in bfloat16 or wider, within the bound.
A program may use at most 192 MiB of HBM per device.

v0:
```python
import math

import jax
import jax.numpy as jnp
from jax import lax
from jax.sharding import PartitionSpec as P

HD = 64
L = 512


def norm_rows(values, gain_vec, bias_vec):
    row_mean = jnp.mean(values, axis=-1, keepdims=True)
    centred = values - row_mean
    variance = jnp.mean(centred * centred, axis=-1, keepdims=True)
    return centred * lax.rsqrt(variance + 1e-05) * gain_vec + bias_vec


def exact_gelu(values):
    return jax.nn.gelu(values, approximate=False)


def segment_ids(lengths):
    bounds = jnp.cumsum(lengths, axis=1)
    positions = jnp.arange(L, dtype=jnp.int32)
    return jnp.sum((positions[None, :, None] >= bounds[:, None, :]).astype(jnp.int32), axis=2)


def local(
    tokens,
    segment_lengths,
    gain_one,
    shift_one,
    qkv_weight,
    qv_bias,
    out_weight,
    out_bias,
    gain_two,
    shift_two,
    up_weight,
    up_bias,
    down_weight,
    down_bias,
    cotangent,
):
    tok_rows = tokens.astype(jnp.float32)
    seg_ids = segment_ids(segment_lengths)
    seq_count = seg_ids.shape[0]
    last_segment = segment_lengths.shape[1] - 1
    same_segment = (seg_ids[:, :, None] == seg_ids[:, None, :])[:, None]
    keep_row = (seg_ids < last_segment).astype(jnp.float32).reshape(seq_count * L, 1)
    head_width = out_weight.shape[0]
    head_count = head_width // HD
    head_shape = (seq_count, L, head_count, HD)
    score_scale = 1.0 / math.sqrt(HD)
    normed_one, norm_one_back = jax.vjp(norm_rows, tok_rows, gain_one, shift_one)
    rows_one = lax.all_gather(normed_one.astype(jnp.bfloat16), "mp", axis=0, tiled=True)
    projected = jnp.einsum("rd,cde->cre", rows_one, qkv_weight, preferred_element_type=jnp.float32)
    query_low = (projected[0] + qv_bias[0]).astype(jnp.bfloat16).reshape(head_shape)
    key_low = projected[1].astype(jnp.bfloat16).reshape(head_shape)
    value_low = (projected[2] + qv_bias[1]).astype(jnp.bfloat16).reshape(head_shape)

    def masked_scores():
        raw_scores = (
            jnp.einsum("sqhd,skhd->shqk", query_low, key_low, preferred_element_type=jnp.float32)
            * score_scale
        )
        return jnp.where(same_segment, raw_scores, -1000000000.0)

    scores = masked_scores()
    row_max = jnp.max(scores, axis=-1, keepdims=True)
    shifted = jnp.exp(scores - row_max)
    exp_total = jnp.sum(shifted, axis=-1, keepdims=True)
    log_total = row_max + jnp.log(exp_total)
    attended = jnp.einsum(
        "shqk,skhd->sqhd",
        (shifted / exp_total).astype(jnp.bfloat16),
        value_low,
        preferred_element_type=jnp.float32,
    )
    attended_low = (attended.reshape(seq_count * L, head_width) * keep_row).astype(jnp.bfloat16)
    row_block = attended_low
    attention_part = lax.psum_scatter(
        jnp.dot(row_block, out_weight, preferred_element_type=jnp.float32),
        "mp",
        scatter_dimension=0,
        tiled=True,
    )
    mixed_rows = tok_rows + attention_part + out_bias
    normed_two, norm_two_back = jax.vjp(norm_rows, mixed_rows, gain_two, shift_two)
    rows_two = lax.all_gather(normed_two.astype(jnp.bfloat16), "mp", axis=0, tiled=True)
    hidden = jnp.dot(rows_two, up_weight, preferred_element_type=jnp.float32) + up_bias
    active, gelu_back = jax.vjp(exact_gelu, hidden)
    active_low = active.astype(jnp.bfloat16)
    row_block = active_low
    layer_output = (
        mixed_rows
        + lax.psum_scatter(
            jnp.dot(row_block, down_weight, preferred_element_type=jnp.float32).astype(
                jnp.bfloat16
            ),
            "mp",
            scatter_dimension=0,
            tiled=True,
        ).astype(jnp.float32)
        + down_bias
    )
    cot_rows = cotangent.astype(jnp.float32)
    cot_gathered = lax.all_gather(cotangent, "mp", axis=0, tiled=True)
    down_weight_grad = jnp.einsum(
        "rf,rd->fd", active_low, cot_gathered, preferred_element_type=jnp.float32
    )
    active_grad = jnp.einsum(
        "rd,fd->rf", cot_gathered, down_weight, preferred_element_type=jnp.float32
    )
    (hidden_grad,) = gelu_back(active_grad)
    hidden_grad_low = hidden_grad.astype(jnp.bfloat16)
    up_bias_grad = jnp.sum(hidden_grad_low, axis=0, dtype=jnp.float32)
    up_weight_grad = jnp.einsum(
        "rd,rf->df", rows_two, hidden_grad_low, preferred_element_type=jnp.float32
    )
    row_block = hidden_grad_low
    normed_two_grad = lax.psum_scatter(
        jnp.einsum("rf,df->rd", row_block, up_weight, preferred_element_type=jnp.float32),
        "mp",
        scatter_dimension=0,
        tiled=True,
    )
    mixed_norm_grad, gain_two_grad, shift_two_grad = norm_two_back(normed_two_grad)
    mixed_grad = cot_rows + mixed_norm_grad
    mixed_grad_low = lax.all_gather(mixed_grad.astype(jnp.bfloat16), "mp", axis=0, tiled=True)
    out_weight_grad = jnp.einsum(
        "re,rd->ed", attended_low, mixed_grad_low, preferred_element_type=jnp.float32
    )
    attended_grad = jnp.einsum(
        "rd,ed->re", mixed_grad_low, out_weight, preferred_element_type=jnp.float32
    )
    attended_grad = (attended_grad.astype(jnp.bfloat16) * keep_row.astype(jnp.bfloat16)).reshape(
        head_shape
    )
    weights_grad = jnp.einsum(
        "sqhd,skhd->shqk", attended_grad, value_low, preferred_element_type=jnp.float32
    )
    softmax_weights = jnp.exp(masked_scores() - log_total)
    weights_low = softmax_weights.astype(jnp.bfloat16)
    value_grad = jnp.einsum(
        "shqk,sqhd->skhd", weights_low, attended_grad, preferred_element_type=jnp.float32
    ).astype(jnp.bfloat16)
    row_dot = jnp.sum(softmax_weights * weights_grad, axis=-1, keepdims=True)
    score_grad = (softmax_weights * (weights_grad - row_dot)).astype(jnp.bfloat16) * score_scale
    query_grad = jnp.einsum(
        "shqk,skhd->sqhd", score_grad, key_low, preferred_element_type=jnp.float32
    ).astype(jnp.bfloat16)
    key_grad = jnp.einsum(
        "shqk,sqhd->skhd", score_grad, query_low, preferred_element_type=jnp.float32
    ).astype(jnp.bfloat16)
    stacked_grad = jnp.stack([query_grad, key_grad, value_grad]).reshape(
        3, seq_count * L, head_width
    )
    qkv_weight_grad = jnp.einsum(
        "rd,cre->cde", rows_one, stacked_grad, preferred_element_type=jnp.float32
    )
    column_sums = jnp.sum(stacked_grad, axis=1, dtype=jnp.float32)
    qv_bias_grad = jnp.stack([column_sums[0], column_sums[2]])
    row_block = stacked_grad
    normed_one_grad = lax.psum_scatter(
        jnp.einsum("cre,cde->rd", row_block, qkv_weight, preferred_element_type=jnp.float32).astype(
            jnp.bfloat16
        ),
        "mp",
        scatter_dimension=0,
        tiled=True,
    ).astype(jnp.float32)
    token_norm_grad, gain_one_grad, shift_one_grad = norm_one_back(normed_one_grad)
    token_grad = mixed_grad + token_norm_grad
    gain_one_grad, shift_one_grad, gain_two_grad, shift_two_grad, out_bias_grad, down_bias_grad = (
        lax.psum(
            (
                gain_one_grad,
                shift_one_grad,
                gain_two_grad,
                shift_two_grad,
                jnp.sum(mixed_grad, axis=0),
                jnp.sum(cot_rows, axis=0),
            ),
            ("dp", "mp"),
        )
    )
    (
        qkv_weight_grad,
        qv_bias_grad,
        out_weight_grad,
        up_weight_grad,
        up_bias_grad,
        down_weight_grad,
    ) = lax.psum(
        (
            qkv_weight_grad,
            qv_bias_grad,
            out_weight_grad,
            up_weight_grad,
            up_bias_grad,
            down_weight_grad,
        ),
        "dp",
    )
    return (
        layer_output,
        token_grad,
        gain_one_grad,
        shift_one_grad,
        qkv_weight_grad,
        qv_bias_grad,
        out_weight_grad,
        out_bias_grad,
        gain_two_grad,
        shift_two_grad,
        up_weight_grad,
        up_bias_grad,
        down_weight_grad,
        down_bias_grad,
    )


def solution(mesh):
    in_specs = (
        P(("dp", "mp"), None),
        P("dp", None),
        P(),
        P(),
        P(None, None, "mp"),
        P(None, "mp"),
        P("mp", None),
        P(),
        P(),
        P(),
        P(None, "mp"),
        P("mp"),
        P("mp", None),
        P(),
        P(("dp", "mp"), None),
    )
    out_specs = (
        P(("dp", "mp"), None),
        P(("dp", "mp"), None),
        P(),
        P(),
        P(None, None, "mp"),
        P(None, "mp"),
        P("mp", None),
        P(),
        P(),
        P(),
        P(None, "mp"),
        P("mp"),
        P("mp", None),
        P(),
    )
    return jax.shard_map(local, mesh=mesh, in_specs=in_specs, out_specs=out_specs, check_vma=False)
```

profile of v0, /device:TPU:0, one launch (start us, length us, event | category | flops | bytes accessed | tf_op | source)
XLA Modules:
  0.0 743.9 jit_solution(7816106143241797058)
XLA Ops:
  13.9 30.1 %all-gather.5.cloned.1.call-done = bf16[2048,768]{1,0:T(8,128)(2,1)} async-done(((bf16[512,768]{1,0:T(8,128)(2,1)}), bf16[2048,768]{1,0:T(8,128)(2,1)}) %all-gather.5.cloned.1.call-update) | async-done | bytes 3145744 | tf_op jit(solution)/shard_map/all_gather | solution.py:57
  44.0 4.1 fusion.121
  53.3 3.4 squeeze.7
  56.8 3.1 squeeze.8
  59.9 7.9 %fusion.3 = (f32[4,3,512]{2,1,0:T(4,128)S(1)}, f32[4,3,512,512]{2,3,1,0:T(8,128)}) fusion(pred[4,512,512]{1,2,0:T(8,128)(4,1)S(1)} %broadcast_compare_fusion, bf16[4,512,3,64]{1,0,3,2:T(4,128)(2,1)S(1)} %convert_element_type.115, f32[4,512,3,64]{1,0,3,2:T(4,128)} %squeeze.8, f32[3,64]{1,0:T(4,128)S(1)} %add.140), kind=kOutput, calls=%fused_computation.10 | convolution fusion | flops 412870656 | bytes 16016128 | tf_op jit(solution)/shard_map/sqhd,skhd->shqk/dot_general | solution.py:65
  67.9 7.5 %fusion.2 = f32[4,3,512]{2,1,0:T(4,128)S(1)} fusion(f32[4,3,512,512]{2,3,1,0:T(8,128)} %get-tuple-element.51, f32[4,3,512]{2,1,0:T(4,128)S(1)} %get-tuple-element.50, pred[4,512,512]{1,2,0:T(8,128)(4,1)S(1)} %broadcast_compare_fusion), kind=kLoop, calls=%fused_computation.8 | loop fusion | flops 12576768 | bytes 13680640 | tf_op jit(solution)/shard_map/reduce_sum | solution.py:73
  75.4 7.2 fusion.55
  85.4 3.7 fusion.90
  89.1 58.9 %reduce-scatter.5.cloned.1.call-done = f32[512,768]{1,0:T(8,128)} async-done(((f32[2048,768]{1,0:T(8,128)}), f32[512,768]{1,0:T(8,128)}) %reduce-scatter.5.cloned.1.call-update) | async-done | bytes 1572880 | tf_op jit(solution)/shard_map/reduce_scatter | solution.py:83
  153.8 28.0 %all-gather.7.cloned.1.call-done = bf16[2048,768]{1,0:T(8,128)(2,1)} async-done(((bf16[512,768]{1,0:T(8,128)(2,1)}), bf16[2048,768]{1,0:T(8,128)(2,1)}) %all-gather.7.cloned.1.call-update) | async-done | bytes 3145744 | tf_op jit(solution)/shard_map/all_gather | solution.py:91
  181.9 7.4 fusion.122
  189.3 22.5 %all-gather.9.cloned.1.call-done = bf16[2048,768]{1,0:T(8,128)(2,1)} async-done(((bf16[512,768]{1,0:T(8,128)(2,1)}), bf16[2048,768]{1,0:T(8,128)(2,1)}) %all-gather.9.cloned.1.call-update) | async-done | bytes 3145744 | tf_op jit(solution)/shard_map/all_gather | solution.py:109
  211.8 20.5 %convert_reduce_fusion = (f32[768]{0:T(1024)}, bf16[2048,768]{1,0:T(8,128)(2,1)S(1)}, f32[2048,768]{1,0:T(8,128)}) fusion(f32[2048,768]{1,0:T(8,128)} %fusion.122, f32[768]{0:T(1024)} %param.26, bf16[2048,768]{1,0:T(8,128)(2,1)} %all-gather.9.cloned.1.call-done, bf16[768,768]{1,0:T(8,128)(2,1)S(1)} %copy-done), kind=kOutput, calls=%fused_computation.14 | convolution fusion | flops 2533883136 | bytes 20060160 | tf_op jit(solution)/shard_map/rd,fd->rf/dot_general | solution.py:113
  234.0 4.5 fusion.123
  238.6 5.5 multiply_convert_fusion.1
  245.9 4.0 convolution_convert_fusion
  249.9 47.6 %reduce-scatter.9.cloned.1.call-done = f32[512,768]{1,0:T(8,128)} async-done(((f32[2048,768]{1,0:T(8,128)}), f32[512,768]{1,0:T(8,128)}) %reduce-scatter.9.cloned.1.call-update) | async-done | bytes 1572880 | tf_op jit(solution)/shard_map/reduce_scatter | solution.py:123
  301.5 36.4 %reduce-scatter.7.cloned.1.call-done = bf16[512,768]{1,0:T(8,128)(2,1)} async-done(((bf16[2048,768]{1,0:T(8,128)(2,1)}), bf16[512,768]{1,0:T(8,128)(2,1)}) %reduce-scatter.7.cloned.1.call-update) | async-done | bytes 786448 | tf_op jit(solution)/shard_map/reduce_scatter | solution.py:98
  337.9 3.6 fusion.116
  343.9 28.5 %all-gather.11.cloned.1.call-done = bf16[2048,768]{1,0:T(8,128)(2,1)} async-done(((bf16[512,768]{1,0:T(8,128)(2,1)}), bf16[2048,768]{1,0:T(8,128)(2,1)}) %all-gather.11.cloned.1.call-update) | async-done | bytes 3145744 | tf_op jit(solution)/shard_map/all_gather | solution.py:131
  377.0 8.3 %fusion.84 = f32[4,3,512,512]{2,3,1,0:T(8,128)} fusion(bf16[4,512,3,64]{1,0,3,2:T(4,128)(2,1)} %reshape.161, f32[4,512,3,64]{1,0,3,2:T(4,128)} %squeeze.7, f32[3,64]{1,0:T(4,128)S(1)} %add.137), kind=kOutput, calls=%fused_computation.94 | convolution fusion | flops 403439616 | bytes 14942976 | tf_op jit(solution)/shard_map/sqhd,skhd->shqk/dot_general | solution.py:141
  385.3 7.6 %fusion.69 = bf16[4,512,3,64]{1,3,2,0:T(8,128)(2,1)} fusion(f32[4,3,512,512]{2,3,1,0:T(8,128)} %get-tuple-element.51, f32[4,3,512]{2,1,0:T(4,128)S(1)} %log_add_fusion, pred[4,512,512]{1,2,0:T(8,128)(4,1)S(1)} %copy-done.7, bf16[4,512,3,64]{1,0,3,2:T(4,128)(2,1)S(1)} %copy-done.15), kind=kOutput, calls=%fused_computation.89 | convolution fusion | flops 415629312 | bytes 15228928 | tf_op jit(solution)/shard_map/shqk,sqhd->skhd/dot_general | solution.py:146
  392.8 21.0 %fusion.72 = bf16[4,512,3,64]{1,3,2,0:T(8,128)(2,1)} fusion(f32[4,3,512,512]{2,3,1,0:T(8,128)} %fusion.84, f32[4,3,512,512]{2,3,1,0:T(8,128)} %get-tuple-element.51, f32[4,3,512]{2,1,0:T(4,128)S(1)} %log_add_fusion, pred[4,512,512]{1,2,0:T(8,128)(4,1)S(1)} %copy-done.7, f32[4,512,3,64]{1,0,3,2:T(4,128)} %squeeze.8, f32[3,64]{1,0:T(4,128)S(1)} %copy-done.35), kind=kOutput, calls=%fused_computation.90 | convolution fusion | flops 447879680 | bytes 28599040 | tf_op jit(solution)/shard_map/shqk,sqhd->skhd/dot_general | solution.py:154
  413.9 20.8 %fusion.77 = bf16[4,512,3,64]{1,3,2,0:T(8,128)(2,1)} fusion(f32[4,3,512,512]{2,3,1,0:T(8,128)} %fusion.84, f32[4,3,512,512]{2,3,1,0:T(8,128)} %get-tuple-element.51, f32[4,3,512]{2,1,0:T(4,128)S(1)} %log_add_fusion, pred[4,512,512]{1,2,0:T(8,128)(4,1)S(1)} %copy-done.7, bf16[4,512,3,64]{1,0,3,2:T(4,128)(2,1)} %copy-done.14), kind=kOutput, calls=%fused_computation.91 | convolution fusion | flops 447093248 | bytes 27811840 | tf_op jit(solution)/shard_map/shqk,skhd->sqhd/dot_general | solution.py:151
  450.0 4.0 bitcast_convert_fusion
  454.4 7.1 fusion.124
  461.5 4.2 fusion.125
  467.5 3.2 fusion.52
  474.0 22.2 %all-reduce.1 = (f32[2,192]{1,0:T(2,128)}, f32[768]{0:T(1024)}) all-reduce(f32[2,192]{1,0:T(2,128)} %pad_maximum_fusion, f32[768]{0:T(1024)} %get-tuple-element.37), channel_id=1, replica_groups=mesh['dp'=8,'mp'=4] {'dp'}, use_global_device_ids=true, to_apply=%region_23.24 | all-reduce | flops 1152 | bytes 9216 | tf_op jit(solution)/shard_map/psum | solution.py:196
  501.3 3.3 convert_reduce_fusion.4
  504.6 42.3 %all-reduce = (f32[768]{0:T(1024)}, f32[768]{0:T(1024)}, f32[768]{0:T(1024)}, f32[768]{0:T(1024)}, f32[768]{0:T(1024)}, /*index=5*/f32[768]{0:T(1024)}) all-reduce(f32[768]{0:T(1024)} %get-tuple-element.16, f32[768]{0:T(1024)} %get-tuple-element.21, f32[768]{0:T(1024)} %get-tuple-element.20, ...), channel_id=1, replica_groups=mesh['dp'=8,'mp'=4] {'dp','mp'}, use_global_device_ids=true, to_apply=%region_18.19 | all-reduce | flops 4608 | bytes 36864 | tf_op jit(solution)/shard_map/psum | solution.py:177
  546.9 183.4 %all-reduce.5.cloned.1.call-done = (f32[3,768,192]{1,2,0:T(8,128)}, f32[192,768]{1,0:T(8,128)}, f32[768,768]{1,0:T(8,128)}, f32[768,768]{1,0:T(8,128)}) async-done(((f32[3,768,192]{1,2,0:T(8,128)}, f32[192,768]{1,0:T(8,128)}, f32[768,768]{1,0:T(8,128)}, f32[768,768]{1,0:T(8,128)}), (f32[3,768,192]{1,2,0:T(8,128)}, f32[192,768]{1,0:T(8,128)}, f32[768,768]{1,0:T(8,128)}, ...) | async-done | bytes 7077904 | tf_op jit(solution)/shard_map/psum | solution.py:196
  (169 shorter events, 66.9 us)
Async XLA Ops:
  7.2 204.6 %copy-start = (bf16[768,768]{1,0:T(8,128)(2,1)S(1)}, bf16[768,768]{1,0:T(8,128)(2,1)}, u32[]{:S(2)}) copy-start(bf16[768,768]{1,0:T(8,128)(2,1)} %param.27) | copy-start | bytes 3538948
  7.2 36.8 %all-gather.5.cloned.1.call-start = ((), (), s32[]{:S(2)}) async-start(), calls=%async_computation.4 | async-start | bytes 3932160 | tf_op jit(solution)/shard_map/all_gather | solution.py:57
  8.7 39.5 %copy-start.28 = (f32[512]{0:T(512)}, f32[512]{0:T(512)S(1)}, u32[]{:S(2)}) copy-start(f32[512]{0:T(512)S(1)} %broadcast_multiply_fusion.1) | copy-start | bytes 6148
  10.2 38.0 %copy-start.36 = (f32[512]{0:T(512)}, f32[512]{0:T(512)S(1)}, u32[]{:S(2)}) copy-start(f32[512]{0:T(512)S(1)} %fusion.46) | copy-start | bytes 6148
  10.2 38.0 %copy-start.31 = (f32[512]{0:T(512)}, f32[512]{0:T(512)S(1)}, u32[]{:S(2)}) copy-start(f32[512]{0:T(512)S(1)} %fusion.95) | copy-start | bytes 6148
  12.6 135.5 %reduce-scatter.5.cloned.1.call-start = ((), (), s32[]{:S(2)}) async-start(), calls=%async_computation.5 | async-start | bytes 7864320 | tf_op jit(solution)/shard_map/reduce_scatter | solution.py:83
  12.9 47.0 %copy-start.34 = (f32[3,64]{1,0:T(4,128)}, f32[3,64]{1,0:T(4,128)S(1)}, u32[]{:S(2)}) copy-start(f32[3,64]{1,0:T(4,128)S(1)} %add.140) | copy-start | bytes 2308
  13.9 61.4 %copy-start.6 = (pred[4,512,512]{1,2,0:T(8,128)(4,1)}, pred[4,512,512]{1,2,0:T(8,128)(4,1)S(1)}, u32[]{:S(2)}) copy-start(pred[4,512,512]{1,2,0:T(8,128)(4,1)S(1)} %broadcast_compare_fusion) | copy-start | bytes 3145732
  67.8 7.5 %copy-start.22 = (f32[4,3,512]{2,1,0:T(4,128)}, f32[4,3,512]{2,1,0:T(4,128)S(1)}, u32[]{:S(2)}) copy-start(f32[4,3,512]{2,1,0:T(4,128)S(1)} %get-tuple-element.50) | copy-start | bytes 73732
  67.9 7.5 %copy-start.11 = (f32[4,512,3,64]{1,0,3,2:T(4,128)S(1)}, f32[4,512,3,64]{1,0,3,2:T(4,128)}, u32[]{:S(2)}) copy-start(f32[4,512,3,64]{1,0,3,2:T(4,128)} %squeeze.7) | copy-start | bytes 4718596
  75.4 7.2 copy-start.26
  89.1 59.0 %copy-start.1 = (bf16[512,768]{1,0:T(8,128)(2,1)S(1)}, bf16[512,768]{1,0:T(8,128)(2,1)}, u32[]{:S(2)}) copy-start(bf16[512,768]{1,0:T(8,128)(2,1)} %param.15) | copy-start | bytes 2359300
  89.1 59.0 %copy-start.41 = (f32[768]{0:T(1024)S(1)}, f32[768]{0:T(1024)}, u32[]{:S(2)}) copy-start(f32[768]{0:T(1024)} %param.22) | copy-start | bytes 9220
  89.1 92.8 %all-gather.7.cloned.1.call-start = ((), (), s32[]{:S(2)}) async-start(), calls=%async_computation.6 | async-start | bytes 3932160 | tf_op jit(solution)/shard_map/all_gather | solution.py:91
  153.2 58.6 %all-gather.9.cloned.1.call-start = ((), (), s32[]{:S(2)}) async-start(), calls=%async_computation.8 | async-start | bytes 3932160 | tf_op jit(solution)/shard_map/all_gather | solution.py:109
  153.8 143.8 %reduce-scatter.9.cloned.1.call-start = ((), (), s32[]{:S(2)}) async-start(), calls=%async_computation.9 | async-start | bytes 7864320 | tf_op jit(solution)/shard_map/reduce_scatter | solution.py:123
  211.8 22.2 %copy-start.46 = (bf16[768,768]{1,0:T(8,128)(2,1)S(1)}, bf16[768,768]{1,0:T(8,128)(2,1)}, u32[]{:S(2)}) copy-start(bf16[768,768]{1,0:T(8,128)(2,1)} %param.25) | copy-start | bytes 3538948
  238.6 99.3 %reduce-scatter.7.cloned.1.call-start = ((), (), s32[]{:S(2)}) async-start(), calls=%async_computation.7 | async-start | bytes 3932160 | tf_op jit(solution)/shard_map/reduce_scatter | solution.py:98
  249.9 122.6 %all-gather.11.cloned.1.call-start = ((), (), s32[]{:S(2)}) async-start(), calls=%async_computation.10 | async-start | bytes 3932160 | tf_op jit(solution)/shard_map/all_gather | solution.py:131
  341.5 31.0 %copy-start.25 = (bf16[192,768]{1,0:T(8,128)(2,1)S(1)}, bf16[192,768]{1,0:T(8,128)(2,1)}, u32[]{:S(2)}) copy-start(bf16[192,768]{1,0:T(8,128)(2,1)} %param.21) | copy-start | bytes 884740
  343.8 152.4 %reduce-scatter.11.cloned.1.call-start = ((), (), s32[]{:S(2)}) async-start(), calls=%async_computation.11 | async-start | bytes 3932160 | tf_op jit(solution)/shard_map/reduce_scatter | solution.py:166
  377.0 8.3 %copy-start.7 = (pred[4,512,512]{1,2,0:T(8,128)(4,1)S(1)}, pred[4,512,512]{1,2,0:T(8,128)(4,1)}, u32[]{:S(2)}) copy-start(pred[4,512,512]{1,2,0:T(8,128)(4,1)} %copy-done.6) | copy-start | bytes 3145732
  377.0 8.3 %copy-start.15 = (bf16[4,512,3,64]{1,0,3,2:T(4,128)(2,1)S(1)}, bf16[4,512,3,64]{1,0,3,2:T(4,128)(2,1)}, u32[]{:S(2)}) copy-start(bf16[4,512,3,64]{1,0,3,2:T(4,128)(2,1)} %reshape.161) | copy-start | bytes 2359300
  385.3 7.6 %copy-start.35 = (f32[3,64]{1,0:T(4,128)S(1)}, f32[3,64]{1,0:T(4,128)}, u32[]{:S(2)}) copy-start(f32[3,64]{1,0:T(4,128)} %copy-done.34) | copy-start | bytes 2308
  454.1 276.3 %all-reduce.5.cloned.1.call-start = ((), (), s32[]{:S(2)}) async-start(), calls=%async_computation.12 | async-start | bytes 14155776 | tf_op jit(solution)/shard_map/psum | solution.py:196
  454.4 7.1 copy-start.17
  454.4 7.1 copy-start.45
  470.7 25.5 %copy-start.29 = (f32[512]{0:T(512)S(1)}, f32[512]{0:T(512)}, u32[]{:S(2)}) copy-start(f32[512]{0:T(512)} %copy-done.28) | copy-start | bytes 6148
  470.7 25.5 %copy-start.30 = (f32[768]{0:T(1024)S(1)}, f32[768]{0:T(1024)}, u32[]{:S(2)}) copy-start(f32[768]{0:T(1024)} %param.17) | copy-start | bytes 9220
  470.7 27.9 %copy-start.37 = (f32[512]{0:T(512)S(1)}, f32[512]{0:T(512)}, u32[]{:S(2)}) copy-start(f32[512]{0:T(512)} %copy-done.36) | copy-start | bytes 6148
  470.7 27.9 %copy-start.32 = (f32[512]{0:T(512)S(1)}, f32[512]{0:T(512)}, u32[]{:S(2)}) copy-start(f32[512]{0:T(512)} %copy-done.31) | copy-start | bytes 6148
  470.7 30.6 %copy-start.5 = (f32[512,768]{1,0:T(8,128)S(1)}, f32[512,768]{1,0:T(8,128)}, u32[]{:S(2)}) copy-start(f32[512,768]{1,0:T(8,128)} %copy-done.4) | copy-start | bytes 4718596
  (26 other events, 82.1 us)
Sparse Core Ops, SparseCore 0:
  12.7 31.2 all-gather.4
  89.2 58.8 reduce-scatter.4
  153.3 28.4 all-gather.6
  183.3 28.4 all-gather.8
  238.7 58.8 reduce-scatter.8
  299.9 37.8 reduce-scatter.6
  343.9 28.4 all-gather.10
  454.2 37.8 reduce-scatter.10
  497.7 232.6 all-reduce.4
where the time goes:
time: 753 us; the launch traced here: 744 us
  waiting for transfers between devices  436 us (58%)
  matrix products  140 us (19%)
  blocking collectives  64.5 us (9%)
  local copies, waits for them, and re-layouts  43.9 us (6%)
  other arithmetic  43.5 us (6%)
  between operations  14.8 us (2%)
    psum x1, waiting for transfers between devices, local(): lax.psum((qkv_weight_grad, qv_bias_grad, out_weight_grad, up_weight_grad,...  183 us
    reduce_scatter x1, waiting for transfers between devices, local(): lax.psum_scatter(jnp.dot(row_block, out_weight, preferred_element_type=jn...  58.9 us
    reduce_scatter x1, waiting for transfers between devices, local(): lax.psum_scatter(jnp.einsum('rf,df->rd', row_block, up_weight, preferred_...  47.6 us
    psum x1, blocking collectives, local(): lax.psum((gain_one_grad, shift_one_grad, gain_two_grad, shift_two_grad, j...  42.3 us
    reduce_scatter x1, waiting for transfers between devices, local(): lax.psum_scatter(jnp.dot(row_block, down_weight, preferred_element_type=j...  36.4 us
    all_gather x1, waiting for transfers between devices, local(): lax.all_gather(normed_one.astype(jnp.bfloat16), 'mp', axis=0, tiled=True)  30.1 us
    all_gather x1, waiting for transfers between devices, local(): lax.all_gather(mixed_grad.astype(jnp.bfloat16), 'mp', axis=0, tiled=True)  28.5 us
    all_gather x1, waiting for transfers between devices, local(): lax.all_gather(normed_two.astype(jnp.bfloat16), 'mp', axis=0, tiled=True)  28 us
  transfers between devices with their start and end apart: 9, of which 8 were waited for; matrix products, arithmetic and copies ran while one was open for 7% of the time, Pallas kernels for 0%

commit v1 on v0

v1 whole, which is shorter than its diff:
```python
import functools
import math

import jax
import jax.numpy as jnp
from jax import lax
from jax.experimental import pallas as pl
from jax.experimental.pallas import tpu as pltpu
from jax.sharding import PartitionSpec as P

MESH = pl.DeviceIdType.MESH
F32, BF16 = jnp.float32, jnp.bfloat16
HD = 64
EPS = 1e-05
CHUNK = 128
INV_SQRT2 = 1.0 / math.sqrt(2.0)
INV_SQRT2PI = 1.0 / math.sqrt(2.0 * math.pi)


def dot(a, b, dims):
    return lax.dot_general(a, b, (dims, ((), ())), preferred_element_type=F32)


def nn(a, b):
    return dot(a, b, ((1,), (0,)))


def nt(a, b):
    return dot(a, b, ((1,), (1,)))


def tn(a, b):
    return dot(a, b, ((0,), (0,)))


def loop(n, fn):
    lax.fori_loop(0, n, lambda i, c: (fn(i), c)[1], 0)


def flip(value, bit):
    return value + bit * (1 - 2 * ((value // bit) % 2))


def body(
    n_dp,
    lens, tok, cot, g1, s1, ob, g2, s2, db, bias, wq_in, wo_in, wu_in, wd_in,
    lo, tg, gsum, small, wd_full,
    wq, wo, wu, wdbuf, biasg, n1, q, k, v, p, dsb, att, mixed, mg, n2, mgl, act, gp, mask,
    csend, crecv, xsend, keep, xrecv, yrecv, zrecv, fin, orecv, srecv,
    own_sem, ag_s, ag_r, b_s, b_r, wd_sem, c_s, c_r, credit, x_s, x_r, y_s, y_r, z_s, z_r,
    a_s, a_r, e_s, e_r, l_s, o_s, o_r, v_s, v_r,
):
    rows, d = tok.shape
    hw = wo_in.shape[0]
    ff = wu_in.shape[1]
    half_w = 2 * hw
    dp, mp = lax.axis_index("dp"), lax.axis_index("mp")
    x, c = mp // 2, mp % 2
    y, zz = dp % 2, dp // 2
    inner = min(n_dp, 8)
    nz = inner // 2
    n_out = n_dp // inner
    z1, zi, base = zz % 2, zz % nz, dp - dp % inner
    sib, xn = flip(mp, 1), flip(mp, 2)
    yn, zn = flip(dp, 1), flip(dp, 2)
    m_x, m_sx = xn, flip(xn, 1)
    groups = 3
    piece = CHUNK // 2 // nz
    per_group = d // CHUNK
    n_chunks = groups * per_group

    def rc(src, dst, ss, rs, dev):
        return pltpu.make_async_remote_copy(
            src_ref=src, dst_ref=dst, send_sem=ss, recv_sem=rs, device_id=dev, device_id_type=MESH
        )

    z_devs = [base + 2 * ((zi + o) % nz) + y for o in range(1, nz)]
    o_devs = [(dp + inner * o) % n_dp for o in range(1, n_out)]
    bits = [1 << b for b in range(n_dp.bit_length() - 1)]
    peers_dp = [yn] + z_devs + o_devs
    peers = [(dp, sib), (dp, xn), (dp, m_sx)] + [(e, mp) for e in peers_dp]

    barrier = pltpu.get_barrier_semaphore()
    for dev in peers:
        pl.semaphore_signal(barrier, inc=1, device_id=dev, device_id_type=MESH)
    pl.semaphore_wait(barrier, len(peers))

    quarter = [hw // 4, hw // 4, d // 4, ff // 4]

    def own(t, r0, n):
        if t == 0:
            return wq_in.at[:, pl.ds(r0, n), :]
        return (wo_in, wu_in, wd_in)[t - 1].at[pl.ds(r0, n), :]

    def full(t, m, r0, n):
        if t == 0:
            return wq.at[:, pl.ds(pl.multiple_of(m * hw + r0, 16), n), :]
        if t == 1:
            return wo.at[pl.ds(pl.multiple_of(m * hw + r0, 16), n), :]
        return (wu, wd_full)[t - 2].at[m, pl.ds(r0, n), :]

    q_own = y + 2 * z1
    q_y, q_z, q_d = (1 - y) + 2 * z1, y + 2 * (1 - z1), (1 - y) + 2 * (1 - z1)

    def reg(t, m, qq, part=None):
        n = quarter[t]
        r0 = pl.multiple_of(qq * n, 16)
        if part is None:
            return full(t, m, r0, n)
        if t == 0:
            ref = wq.at[pl.ds(0, 1)] if part == "y" else wq.at[pl.ds(1, 2)]
            return ref.at[:, pl.ds(pl.multiple_of(m * hw + r0, 16), n), :]
        if t == 1:
            return full(t, m, r0, n)
        return full(t, m, r0 + (0 if part == "y" else n // 2), n // 2)

    def whole(t, m):
        return full(t, m, 0, 4 * quarter[t])

    dev_s, dev_x, dev_y, dev_z = (dp, sib), (dp, xn), (yn, mp), (zn, mp)

    def c_own(t):
        return pltpu.make_async_copy(own(t, 0, 4 * quarter[t]), whole(t, mp), own_sem.at[t])

    def d_own(t):
        return rc(own(t, 0, 4 * quarter[t]), whole(t, mp), ag_s.at[t, 0], ag_r.at[t, 0], dev_s)

    def d_x(t):
        n = quarter[t]
        return rc(own(t, pl.multiple_of(q_own * n, 16), n), reg(t, mp, q_own), ag_s.at[t, 1], ag_r.at[t, 1], dev_x)

    def fwd(t, qq, part, si, ri, dev):
        r = reg(t, m_x, qq, part)
        return rc(r, r, ag_s.at[t, si], ag_r.at[t, ri], dev)

    def d_y(t):
        return fwd(t, q_own, None, 2, 2, dev_y)

    def d_z(t):
        return fwd(t, q_own, None, 3, 3, dev_z)

    def d_s(t, qq, si):
        return fwd(t, qq, None, si, 6, dev_s)

    def d_dz(t):
        return fwd(t, q_y, "z", 6, 4, dev_z)

    def d_dy(t):
        return fwd(t, q_z, "y", 8, 5, dev_y)

    def arrive(region, sem, dev):
        rc(region, region, ag_s.at[0, 0], sem, dev).wait_recv()

    def f1(t):
        arrive(reg(t, m_x, q_own), ag_r.at[t, 1], dev_x)
        d_y(t).start()
        d_z(t).start()
        d_s(t, q_own, 4).start()

    def f2(t):
        arrive(reg(t, m_x, q_y), ag_r.at[t, 2], dev_y)
        if t != 1:
            d_dz(t).start()
        d_s(t, q_y, 5).start()
        arrive(reg(t, m_x, q_z), ag_r.at[t, 3], dev_z)
        d_dy(t).start()
        d_s(t, q_z, 7).start()

    def f3(t):
        if t != 1:
            arrive(reg(t, m_x, q_d, "z"), ag_r.at[t, 4], dev_z)
        arrive(reg(t, m_x, q_d, "y"), ag_r.at[t, 5], dev_y)
        d_s(t, q_d, 9).start()

    def near(t):
        c_own(t).wait()
        arrive(whole(t, sib), ag_r.at[t, 0], dev_s)

    def far(t):
        arrive(whole(t, m_sx), ag_r.at[t, 6], dev_s)

    def sent(t):
        for cp in (d_own(t), d_x(t), d_y(t), d_z(t), d_s(t, q_own, 4), d_s(t, q_y, 5), d_s(t, q_z, 7),
                   d_dy(t), d_s(t, q_d, 9)):
            cp.wait_send()
        if t != 1:
            d_dz(t).wait_send()

    def d_bias(i):
        dev = [sib, xn, m_sx][i]
        return rc(bias, biasg.at[mp], b_s.at[i], b_r.at[i], (dp, dev))

    for t in range(4):
        d_x(t).start()
        d_own(t).start()
        c_own(t).start()
        if t == 0:
            for i in range(3):
                d_bias(i).start()

    def rows_of(ref, r0, n):
        return ref.at[pl.ds(pl.multiple_of(r0, 16), n), :]

    half = CHUNK // 2

    def d_xs(t):
        return rc(rows_of(xsend, t * CHUNK, CHUNK), rows_of(xrecv, t * CHUNK, CHUNK), x_s.at[t], x_r.at[t], dev_x)

    def d_ys(t):
        return rc(rows_of(keep, t * CHUNK + (1 - y) * half, half), rows_of(yrecv, t * half, half),
                  y_s.at[t], y_r.at[t], dev_y)

    def piece_at(t, zj):
        return t * CHUNK + y * half + zj * piece

    def d_zs(t, o):
        j = t * (nz - 1) + o - 1
        return rc(rows_of(keep, piece_at(t, (zi + o) % nz), piece), rows_of(zrecv, j * piece, piece),
                  z_s.at[j], z_r.at[j], (z_devs[o - 1], mp))

    def d_as(t, o):
        j = t * (nz - 1) + o - 1
        return rc(rows_of(fin, t * piece, piece), rows_of(gsum, piece_at(t, zi), piece),
                  a_s.at[j], a_r.at[j], (z_devs[o - 1], mp))

    def d_ar(t, o):
        j = t * (nz - 1) + o - 1
        r = rows_of(gsum, piece_at(t, (zi + nz - o) % nz), piece)
        return rc(r, r, a_s.at[j], a_r.at[j], (z_devs[o - 1], mp))

    def d_os(t, o):
        j = t * (n_out - 1) + o - 1
        return rc(rows_of(fin, t * piece, piece), rows_of(orecv, j * piece, piece),
                  o_s.at[j], o_r.at[j], (o_devs[o - 1], mp))

    def c_ls(t):
        return pltpu.make_async_copy(rows_of(fin, t * piece, piece), rows_of(gsum, piece_at(t, zi), piece), l_s.at[t])

    def d_es(t):
        r = rows_of(gsum, t * CHUNK + y * half, half)
        return rc(r, r, e_s.at[t], e_r.at[t], dev_y)

    def d_er(t):
        r = rows_of(gsum, t * CHUNK + (1 - y) * half, half)
        return rc(r, r, e_s.at[t], e_r.at[t], dev_y)

    def get(ref, r0, n):
        return ref[pl.ds(pl.multiple_of(r0, 16), n), :].astype(F32)

    def put(ref, r0, n, val):
        ref[pl.ds(pl.multiple_of(r0, 16), n), :] = val.astype(BF16)

    def st_y(t):
        d_xs(t).wait_recv()
        r0 = t * CHUNK
        put(keep, r0, CHUNK, get(keep, r0, CHUNK) + get(xrecv, r0, CHUNK))
        d_ys(t).start()

    def st_z(t):
        d_ys(t).wait_recv()
        r0 = t * CHUNK + y * half
        put(keep, r0, half, get(keep, r0, half) + get(yrecv, t * half, half))
        for o in range(1, nz):
            d_zs(t, o).start()

    def st_a(t):
        for o in range(1, nz):
            d_zs(t, o).wait_recv()
        acc = get(keep, piece_at(t, zi), piece)
        for o in range(1, nz):
            acc = acc + get(zrecv, (t * (nz - 1) + o - 1) * piece, piece)
        put(fin, t * piece, piece, acc)
        if n_out == 1:
            st_g(t)
        else:
            for o in range(1, n_out):
                d_os(t, o).start()

    def st_o(t):
        own_part = get(fin, t * piece, piece)
        acc = own_part
        for o in range(1, n_out):
            d_os(t, o).wait_recv()
            d_os(t, o).wait_send()
        me = dp // inner
        acc = jnp.zeros_like(own_part)
        for gidx in range(n_out):
            slot = (me - gidx + n_out) % n_out
            r0 = (t * (n_out - 1) + jnp.maximum(slot, 1) - 1) * piece
            acc = acc + jnp.where(slot == 0, own_part, get(orecv, r0, piece))
        put(fin, t * piece, piece, acc)
        st_g(t)

    def st_g(t):
        c_ls(t).start()
        for o in range(1, nz):
            d_as(t, o).start()

    def st_b(t):
        c_ls(t).wait()
        for o in range(1, nz):
            d_ar(t, o).wait_recv()
        d_es(t).start()

    def st_e(t):
        d_er(t).wait_recv()
        d_xs(t).wait_send()
        d_ys(t).wait_send()
        d_es(t).wait_send()
        for o in range(1, nz):
            d_zs(t, o).wait_send()
            d_as(t, o).wait_send()

    stages = [st_y, st_z, st_a] + ([st_o] if n_out > 1 else []) + [st_b, st_e]

    def tick(t):
        for s in reversed(range(len(stages))):
            u = t - s

            @pl.when(jnp.logical_and(u >= 0, u < n_chunks))
            def _(s=s, u=u):
                stages[s](u)

    def d_c(slot):
        return rc(csend.at[slot], crecv.at[slot], c_s.at[slot], c_r.at[slot], dev_s)

    def m_of(i):
        mx = jnp.where(i % 2 == 0, 1 - x, x)
        mc = jnp.where(i < 2, 1 - c, c)
        return 2 * mx + mc

    small[...] = jnp.zeros_like(small)
    rb = 128

    def ln1(i):
        r = pl.ds(pl.multiple_of(i * rb, rb), rb)
        xv = tok[r, :].astype(F32)
        xc = xv - jnp.mean(xv, axis=-1, keepdims=True)
        inv = lax.rsqrt(jnp.mean(xc * xc, axis=-1, keepdims=True) + EPS)
        n1[r, :] = (xc * inv * g1[...] + s1[...]).astype(BF16)
        small[5:6, :] += jnp.sum(cot[r, :].astype(F32), axis=0, keepdims=True)

    loop(rows // rb, ln1)

    n_seg = lens.shape[1]
    col = lax.broadcasted_iota(jnp.int32, (rows, 1), 0)
    row = lax.broadcasted_iota(jnp.int32, (1, rows), 1)
    seg_col, seg_row = jnp.zeros_like(col), jnp.zeros_like(row)
    bound = jnp.int32(0)
    for j in range(n_seg):
        bound = bound + lens[mp, j]
        seg_col = seg_col + (col >= bound).astype(jnp.int32)
        seg_row = seg_row + (row >= bound).astype(jnp.int32)
    mask[...] = jnp.where(seg_col == seg_row, 0.0, -1000000000.0).astype(F32)
    kept = (seg_col < n_seg - 1).astype(F32)

    biasg[mp] = bias[...]
    for i in range(3):
        d_bias(i).wait()
    bias_sum = biasg[0, 1:3, :] + biasg[1, 1:3, :] + biasg[2, 1:3, :] + biasg[3, 1:3, :]
    small[14:16, :] = bias_sum

    scale = 1.0 / math.sqrt(HD)
    n_pairs = d // (2 * HD)
    per_half = n_pairs // 2
    low_half = lax.broadcasted_iota(jnp.int32, (1, 2 * HD), 1) < HD
    ab = rows // 2

    def lanes_of(i):
        xh = jnp.where(i < per_half, x, 1 - x)
        pair = xh * per_half + i % per_half
        return xh, pair, pl.ds(pl.multiple_of(pair * 2 * HD, 128), 2 * HD)

    def pick(h, val):
        zero = jnp.zeros_like(val)
        return jnp.where(low_half, val, zero) if h == 0 else jnp.where(low_half, zero, val)

    def attn_fwd(i):
        xh, pair, lanes = lanes_of(i)

        @pl.when(i == 0)
        def _():
            near(0)

        @pl.when(i == per_half)
        def _():
            far(0)

        @pl.when(i % per_half == 0)
        def _():
            w_rows = pl.ds(pl.multiple_of(xh * half_w, 128), half_w)
            w_lanes = w_rows
            for cc, ref in enumerate((q, k, v)):
                val = nt(n1[...], wq[cc, w_rows, :])
                if cc == 0:
                    val = val + small[14:15, w_lanes]
                if cc == 2:
                    val = val + small[15:16, w_lanes]
                val = val.astype(BF16)
                if cc == 0:
                    val = val * jnp.asarray(scale, BF16)
                ref[:, w_lanes] = val

        k2, v2 = k[:, lanes], v[:, lanes]
        for r in range(2):
            rs = pl.ds(r * ab, ab)
            q2 = q[rs, lanes]
            outs = []
            for h in range(2):
                sc = nt(pick(h, q2), k2) + mask[rs, :]
                e = jnp.exp(sc - jnp.max(sc, axis=-1, keepdims=True))
                pr = (e * (1.0 / jnp.sum(e, axis=-1, keepdims=True))).astype(BF16)
                p[2 * pair + h, rs, :] = pr
                outs.append(nn(pr, v2))
            o2 = jnp.where(low_half, outs[0], outs[1]) * kept[r * ab:(r + 1) * ab]
            att[rs, lanes] = o2.astype(BF16)

        for at, todo in enumerate(AG_PLAN):
            @pl.when(i == at)
            def _(todo=todo):
                for fn, t in todo:
                    (f1, f2, f3)[fn - 1](t)

    AG_PLAN = [
        [(1, 0)],
        [(2, 0), (1, 1)],
        [(3, 0), (2, 1), (1, 2)],
        [(3, 1), (2, 2), (1, 3)],
        [(3, 2), (2, 3)],
        [(3, 3)],
    ]
    loop(n_pairs, attn_fwd)

    near(1)
    far(1)
    mixed[...] = nn(att[...], wo[...])

    def ln2(i):
        r = pl.ds(pl.multiple_of(i * rb, rb), rb)
        xv = tok[r, :].astype(F32) + mixed[r, :] + ob[...]
        mixed[r, :] = xv
        lo[r, :] = xv + db[...]
        xc = xv - jnp.mean(xv, axis=-1, keepdims=True)
        inv = lax.rsqrt(jnp.mean(xc * xc, axis=-1, keepdims=True) + EPS)
        n2[r, :] = (xc * inv * g2[...] + s2[...]).astype(BF16)

    loop(rows // rb, ln2)

    tile = 256

    def emit_block(g, i, make):
        if g > 0:
            @pl.when(i < 2)
            def _():
                pl.semaphore_wait(credit.at[i], 1)
                d_c(i).wait_send()

        @pl.when(i >= 2)
        def _():
            d_c(i - 2).wait_recv()

        def part(r):
            rr = pl.ds(pl.multiple_of(r * tile, tile), tile)
            res = make(r)

            @pl.when(i < 2)
            def _():
                csend[i, rr, :] = res.astype(BF16)

            @pl.when(i >= 2)
            def _():
                tot = (res + crecv[i - 2, rr, :].astype(F32)).astype(BF16)
                out = pl.ds(pl.multiple_of(g * d + r * tile, tile), tile)

                @pl.when(i == 2)
                def _():
                    xsend[out, :] = tot
                    for cc in range(tile // CHUNK):
                        d_xs(g * per_group + r * (tile // CHUNK) + cc).start()

                @pl.when(i == 3)
                def _():
                    keep[out, :] = tot

        loop(d // tile, part)

        @pl.when(i < 2)
        def _():
            d_c(i).start()

        @pl.when(i >= 2)
        def _():
            pl.semaphore_signal(credit.at[i - 2], inc=1, device_id=dev_s, device_id_type=MESH)

    near(2)
    far(2)

    def ffn1(i):
        m = m_of(i)

        def hid(n):
            nl = pl.ds(pl.multiple_of(n * tile, tile), tile)
            h = nn(n2[...], wu[m, :, nl]) + biasg[m, 0:1, nl]
            phi = 0.5 * (1.0 + lax.erf(h * INV_SQRT2))
            act[m, :, nl] = (h * phi).astype(BF16)
            gp[m, :, nl] = (phi + h * jnp.exp(-0.5 * h * h) * INV_SQRT2PI).astype(BF16)

        loop(ff // tile, hid)

        def make(r):
            rl = pl.ds(pl.multiple_of(r * tile, tile), tile)
            return tn(act[m, :, rl], cot[...])

        emit_block(0, i, make)

    loop(4, ffn1)

    near(3)
    far(3)

    def c_wd(i):
        return pltpu.make_async_copy(wd_full.at[m_of(i)], wdbuf.at[i % 2], wd_sem.at[i % 2])

    c_wd(0).start()
    mg[...] = jnp.zeros_like(mg)

    def ffn2(i):
        m = m_of(i)
        c_wd(i).wait()

        @pl.when(i < 3)
        def _():
            c_wd(i + 1).start()

        s = i % 2

        def hg(n):
            nl = pl.ds(pl.multiple_of(n * tile, tile), tile)
            val = (gp[m, :, nl].astype(F32) * nt(cot[...], wdbuf[s, nl, :])).astype(BF16)
            gp[m, :, nl] = val
            small[pl.ds(8 + m, 1), nl] = jnp.sum(val.astype(F32), axis=0, keepdims=True)

        loop(ff // tile, hg)

        def make(r):
            rl = pl.ds(pl.multiple_of(r * tile, tile), tile)
            return tn(n2[:, rl], gp[m])

        emit_block(1, i, make)

        def back(n):
            nl = pl.ds(pl.multiple_of(n * tile, tile), tile)
            mg[:, nl] += nt(gp[m], wu[m, nl, :])
            lo[:, nl] += nn(act[m], wdbuf[s, :, nl])

        loop(d // tile, back)
        tick(i)

    loop(4, ffn2)

    def ln2b(i):
        r = pl.ds(pl.multiple_of(i * rb, rb), rb)
        xv = mixed[r, :]
        xc = xv - jnp.mean(xv, axis=-1, keepdims=True)
        inv = lax.rsqrt(jnp.mean(xc * xc, axis=-1, keepdims=True) + EPS)
        xh = xc * inv
        dn = mg[r, :]
        small[2:3, :] += jnp.sum(dn * xh, axis=0, keepdims=True)
        small[3:4, :] += jnp.sum(dn, axis=0, keepdims=True)
        gg = dn * g2[...]
        val = cot[r, :].astype(F32) + (
            gg - jnp.mean(gg, axis=-1, keepdims=True) - xh * jnp.mean(gg * xh, axis=-1, keepdims=True)
        ) * inv
        mg[r, :] = val
        mgl[r, :] = val.astype(BF16)
        small[4:5, :] += jnp.sum(val, axis=0, keepdims=True)

    loop(rows // rb, ln2b)

    da = n2

    def dab(n):
        nl = pl.ds(pl.multiple_of(n * tile, tile), tile)
        da[:, nl] = (nt(mgl[...], wo[nl, :]).astype(BF16).astype(F32) * kept).astype(BF16)

    loop(d // tile, dab)
    tick(4)

    def attn_bwd(i):
        xh, pair, lanes = lanes_of((i + per_half) % n_pairs)
        k2, v2 = k[:, lanes], v[:, lanes]
        do2, q2 = da[:, lanes], q[:, lanes]
        dqs, dks, dvs = [], [], []
        for h in range(2):
            dq_rows = []
            for r in range(2):
                rs = slice(r * ab, (r + 1) * ab)
                dpv = nt(pick(h, do2[rs]), v2)
                pr = p[2 * pair + h, pl.ds(r * ab, ab), :].astype(F32)
                t1 = pr * dpv
                ds = (t1 - pr * jnp.sum(t1, axis=-1, keepdims=True)).astype(BF16)
                dsb[pl.ds(r * ab, ab), :] = ds
                dq_rows.append(nn(ds, k2))
            dqs.append(jnp.concatenate(dq_rows, axis=0))
            dks.append(tn(dsb[...], q2))
            dvs.append(tn(p[2 * pair + h], do2))
        dv2 = jnp.where(low_half, dvs[0], dvs[1]).astype(BF16)
        dk2 = jnp.where(low_half, dks[0], dks[1]).astype(BF16)
        dq2 = (jnp.where(low_half, dqs[0], dqs[1]) * scale).astype(BF16)
        q[:, lanes] = dq2
        k[:, lanes] = dk2
        v[:, lanes] = dv2
        small[6:7, lanes] = jnp.sum(dq2.astype(F32), axis=0, keepdims=True)
        small[7:8, lanes] = jnp.sum(dv2.astype(F32), axis=0, keepdims=True)

        @pl.when(i % per_half == per_half - 1)
        def _():
            a = i // per_half
            wl = pl.ds(pl.multiple_of(xh * half_w, 128), half_w)
            pl.semaphore_wait(credit.at[a], 1)
            d_c(a).wait_send()
            for j, (ref, other) in enumerate(((att, mgl), (q, n1), (k, n1), (v, n1))):
                act[pl.ds(0, 2), pl.ds(0, hw), :] = tn(ref[:, wl], other[...]).astype(BF16).reshape(2, hw, d)
                csend[a, j * hw:(j + 1) * hw, :] = act[1 - c, 0:hw, :]
                gp[0 if j < 2 else 1, (j % 2) * hw:(j % 2 + 1) * hw, :] = act[c, 0:hw, :]
            d_c(a).start()
            d_c(a).wait_recv()
            for j in range(4):
                tot = (gp[0 if j < 2 else 1, (j % 2) * hw:(j % 2 + 1) * hw, :].astype(F32)
                       + crecv[a, j * hw:(j + 1) * hw, :].astype(F32)).astype(BF16)

                @pl.when(a == 0)
                def _():
                    xsend[2 * d + j * hw:2 * d + (j + 1) * hw, :] = tot

                @pl.when(a == 1)
                def _():
                    keep[2 * d + j * hw:2 * d + (j + 1) * hw, :] = tot

            @pl.when(a == 0)
            def _():
                for cc in range(per_group):
                    d_xs(2 * per_group + cc).start()

        tick(5 + i)

    loop(n_pairs, attn_bwd)

    def ln1n(n):
        nl = pl.ds(pl.multiple_of(n * tile, tile), tile)
        tg[:, nl] = nn(q[...], wq[0, :, nl]) + nn(k[...], wq[1, :, nl]) + nn(v[...], wq[2, :, nl])

    loop(d // tile, ln1n)

    def ln1b(i):
        r = pl.ds(pl.multiple_of(i * rb, rb), rb)
        xv = tok[r, :].astype(F32)
        xc = xv - jnp.mean(xv, axis=-1, keepdims=True)
        inv = lax.rsqrt(jnp.mean(xc * xc, axis=-1, keepdims=True) + EPS)
        xh = xc * inv
        dn = tg[r, :]
        small[0:1, :] += jnp.sum(dn * xh, axis=0, keepdims=True)
        small[1:2, :] += jnp.sum(dn, axis=0, keepdims=True)
        gg = dn * g1[...]
        tg[r, :] = mg[r, :] + (
            gg - jnp.mean(gg, axis=-1, keepdims=True) - xh * jnp.mean(gg * xh, axis=-1, keepdims=True)
        ) * inv

    loop(rows // rb, ln1b)

    v_devs = [(dp, sib), (dp, xn)] + [(flip(dp, b), mp) for b in bits]

    def d_v(s):
        return rc(small, srecv.at[s], v_s.at[s], v_r.at[s], v_devs[s])

    first = 5 + n_pairs

    def tail(i):
        for s in range(len(v_devs) + 1):
            @pl.when(i == s)
            def _(s=s):
                if s > 0:
                    d_v(s - 1).wait()
                    small[...] += srecv[s - 1]
                if s < len(v_devs):
                    d_v(s).start()

        tick(first + i)

    loop(max(n_chunks + len(stages) - 1 - first, len(v_devs) + 1), tail)
    for slot in range(2):
        d_c(slot).wait_send()
    for t in range(4):
        sent(t)


def layer(n_dp, tokens, lens, g1, s1, wqkv, qvb, wo, ob, g2, s2, wu, ub, wd, db, cot):
    rows, d = tokens.shape
    hw, ff = wo.shape[0], wu.shape[1]
    n_mp = lax.axis_size("mp")
    mp = lax.axis_index("mp")
    inner = min(n_dp, 8)
    nz, n_out = inner // 2, n_dp // inner
    piece = CHUNK // 2 // nz
    nc = 3 * d // CHUNK
    n_small = 2 + n_dp.bit_length() - 1
    heads = d // HD
    vec = lambda a: a.reshape(1, d)
    lane = jnp.arange(d, dtype=jnp.int32)[None, :]
    wide = jnp.concatenate([qvb] * n_mp, axis=1)
    bias = jnp.concatenate(
        [ub.reshape(1, d), jnp.where(lane // hw == mp, wide, 0.0), jnp.zeros((5, d), F32)], axis=0
    )
    wqt = jnp.swapaxes(wqkv, 1, 2)
    vm = pl.BlockSpec(memory_space=pltpu.VMEM)
    hbm = pl.BlockSpec(memory_space=pl.ANY)
    sm = pl.BlockSpec(memory_space=pltpu.SMEM)
    dma = pltpu.SemaphoreType.DMA
    S = jax.ShapeDtypeStruct
    V = pltpu.VMEM
    nzr = max(nc * (nz - 1), 1)
    nor = max(nc * (n_out - 1), 1)
    lo, tg, gsum, small, _ = pl.pallas_call(
        functools.partial(body, n_dp),
        out_shape=(
            S((rows, d), F32), S((rows, d), F32), S((3 * d, d), BF16), S((16, d), F32), S((n_mp, ff, d), BF16),
        ),
        in_specs=[sm] + [vm] * 9 + [hbm] * 4,
        out_specs=(vm, vm, hbm, vm, hbm),
        scratch_shapes=[
            V((3, d, d), BF16), V((d, d), BF16), V((n_mp, d, ff), BF16), V((2, ff, d), BF16), V((n_mp, 8, d), F32),
            V((rows, d), BF16), V((rows, d), BF16), V((rows, d), BF16), V((rows, d), BF16),
            V((heads, rows, rows), BF16), V((rows, rows), BF16), V((rows, d), BF16),
            V((rows, d), F32), V((rows, d), F32), V((rows, d), BF16), V((rows, d), BF16),
            V((n_mp, rows, ff), BF16), V((n_mp, rows, ff), BF16), V((rows, rows), F32),
            V((2, d, d), BF16), V((2, d, d), BF16), V((3 * d, d), BF16), V((3 * d, d), BF16), V((3 * d, d), BF16),
            V((nc * CHUNK // 2, d), BF16), V((nzr * piece, d), BF16), V((nc * piece, d), BF16),
            V((nor * piece, d), BF16), V((n_small, 16, d), F32),
            dma((4,)), dma((4, 10)), dma((4, 7)), dma((3,)), dma((3,)), dma((2,)), dma((2,)), dma((2,)),
            pltpu.SemaphoreType.REGULAR((2,)), dma((nc,)), dma((nc,)), dma((nc,)), dma((nc,)),
            dma((nzr,)), dma((nzr,)), dma((nzr,)), dma((nzr,)), dma((nc,)), dma((nc,)), dma((nc,)),
            dma((nor,)), dma((nor,)), dma((n_small,)), dma((n_small,)),
        ],
        compiler_params=pltpu.CompilerParams(
            collective_id=0, has_side_effects=True, vmem_limit_bytes=67043328
        ),
        name="layer",
    )(lens, tokens, cot, vec(g1), vec(s1), vec(ob), vec(g2), vec(s2), vec(db), bias, wqt, wo, wu, wd)

    f = lambda a: a.astype(F32)
    dqkv = f(jnp.swapaxes(gsum[2 * d + hw:].reshape(3, hw, d), 1, 2))
    qv = lax.dynamic_slice(small, (6, mp * hw), (2, hw))
    upb = lax.dynamic_slice(small, (8 + mp, 0), (1, d)).reshape(d)
    return (
        lo, tg, small[0], small[1], dqkv, qv, f(gsum[2 * d:2 * d + hw]), small[4], small[2], small[3],
        f(gsum[d:2 * d]), upb, f(gsum[:d]), small[5],
    )


def solution(mesh):
    rows = P(("dp", "mp"), None)
    in_specs = (
        rows, P("dp", None), P(), P(), P(None, None, "mp"), P(None, "mp"), P("mp", None), P(), P(), P(),
        P(None, "mp"), P("mp"), P("mp", None), P(), rows,
    )
    out_specs = (
        rows, rows, P(), P(), P(None, None, "mp"), P(None, "mp"), P("mp", None), P(), P(), P(),
        P(None, "mp"), P("mp"), P("mp", None), P(),
    )
    return jax.shard_map(
        functools.partial(layer, mesh.shape["dp"]), mesh=mesh, in_specs=in_specs, out_specs=out_specs, check_vma=False
    )
```

time: 753 us -> 221 us (0.29); the launches traced: 744 us -> 221 us
  waiting for transfers between devices: 436 us -> 0 us
  Pallas kernels: 0 us -> 197 us
  matrix products: 140 us -> 0 us
  blocking collectives: 64.5 us -> 0 us
  other arithmetic: 43.5 us -> 7.3 us
  local copies, waits for them, and re-layouts: 43.9 us -> 15.9 us
  between operations: 14.8 us -> 0.68 us
    pallas_call x0 -> x1, Pallas kernels: none -> 197 us  [layer(): pl.pallas_call(functools.partial(body, n_dp), out_shape=(S((rows, d), F32...]
    psum x1 -> x0, waiting for transfers between devices: 183 us -> none  [local(): lax.psum((qkv_weight_grad, qv_bias_grad, out_weight_grad, up_weight_grad,...]
    reduce_scatter x4 -> x0, waiting for transfers between devices: 143 us -> none  [the longest x1 58.9 us: local(): lax.psum_scatter(jnp.dot(row_block, out_weight, preferred_element_type=jn...]
    dot_general x17 -> x0, matrix products: 136 us -> none  [the longest x1 21 us: local(): jnp.einsum('shqk,sqhd->skhd', score_grad, query_low, preferred_element_ty...]
    all_gather x4 -> x0, waiting for transfers between devices: 109 us -> none  [the longest x1 30.1 us: local(): lax.all_gather(normed_one.astype(jnp.bfloat16), 'mp', axis=0, tiled=True)]
    psum x2 -> x0, blocking collectives: 64.5 us -> none  [the longest x1 42.3 us: local(): lax.psum((gain_one_grad, shift_one_grad, gain_two_grad, shift_two_grad, j...]
    reduce_sum x12 -> x0, other arithmetic: 29.7 us -> none  [the longest x3 7.7 us: norm_rows(): return centred * lax.rsqrt(variance + 1e-05) * gain_vec + bias_vec]
    unnamed x106 -> x8, local copies, waits for them, and re-layouts: 17 us -> 3.12 us
  transfers between devices with their start and end apart: 9 -> 0, of which waited for: 8 -> 0; matrix products, arithmetic and copies ran while one was open for 7% -> 0% of each run, Pallas kernels for 0% -> 0%
where the time goes in v1:
time: 221 us
  Pallas kernels  197 us (89%)
  local copies, waits for them, and re-layouts  15.9 us (7%)
  other arithmetic  7.3 us (3%)
    pallas_call x1, Pallas kernels, layer(): pl.pallas_call(functools.partial(body, n_dp), out_shape=(S((rows, d), F32...  197 us
    reshape x6, local copies, waits for them, and re-layouts, layer(): vec = lambda a: a.reshape(1, d)  7.6 us
    convert_element_type x3, other arithmetic, layer(): f = lambda a: a.astype(F32)  5.71 us

profile of v1, /device:TPU:0, one launch (start us, length us, event | category | flops | bytes accessed | tf_op | source)
XLA Modules:
  0.0 220.7 jit_solution(1446398123638436585)
XLA Ops:
  0.7 0.1 pad.2.clone
  0.8 1.3 reshape.80.g1
  2.0 1.3 reshape.81.s1
  3.3 1.3 reshape.82.ob
  4.6 1.3 reshape.83.g2
  5.8 1.3 reshape.84.s2
  7.1 0.7 reshape.86
  7.8 1.3 reshape.85.db
  9.0 0.9 maximum_select_fusion
  9.9 0.7 maximum_maximum_fusion.bias
  10.6 196.9 %layer.1 = (f32[512,768]{1,0:T(8,128)}, f32[512,768]{1,0:T(8,128)}, bf16[2304,768]{1,0:T(8,128)(2,1)}, f32[16,768]{1,0:T(8,128)}, bf16[4,768,768]{2,1,0:T(8,128)(2,1)}) custom-call(s32[4,8]{1,0:T(4,128)} %lens.1, bf16[512,768]{1,0:T(8,128)(2,1)} %tok.1, bf16[512,768]{1,0:T(8,128)(2,1)} %cot.1, f32[1,768]{1,0:T(1,128)} %reshape.80.g1, f32[1,768]{1,0:T(1,128)} %reshape.81.s1, ...), custom_call_target="tpu_custom_call" | custom-call | tf_op jit(solution)/shard_map/layer/pallas_call | solution.py:723
  207.5 1.4 constant_dynamic-slice_fusion
  208.9 1.6 slice_reduce_fusion
  210.5 1.8 slice_convert_fusion.2
  212.3 0.0 copy-start
  212.3 1.4 slice.32
  213.7 1.4 convert_bitcast_fusion
  215.0 0.0 copy-done
  215.0 0.0 copy-start.2
  215.0 2.5 %slice_convert_fusion = (f32[768,768]{1,0:T(8,128)}, f32[768,768]{1,0:T(8,128)}) fusion(bf16[2304,768]{1,0:T(8,128)(2,1)S(1)} %copy-done), kind=kLoop, calls=%fused_computation.1 | loop fusion | flops 1179648 | bytes 7077888 | tf_op jit(solution)/shard_map/convert_element_type | solution.py:750
  217.6 0.0 copy-start.1
  217.6 0.0 copy-done.2
  217.6 1.1 copy.31
  218.7 0.8 copy-done.1
  219.6 1.1 copy.32
  (2 shorter events, 0.0 us)
Async XLA Ops:
  212.3 2.7 %copy-start = (bf16[2304,768]{1,0:T(8,128)(2,1)S(1)}, bf16[2304,768]{1,0:T(8,128)(2,1)}, u32[]{:S(2)}) copy-start(bf16[2304,768]{1,0:T(8,128)(2,1)} %get-tuple-element.21) | copy-start | bytes 10616836
  215.0 2.6 %copy-start.2 = (f32[512,768]{1,0:T(8,128)S(1)}, f32[512,768]{1,0:T(8,128)}, u32[]{:S(2)}) copy-start(f32[512,768]{1,0:T(8,128)} %get-tuple-element.45) | copy-start | bytes 4718596
  217.6 2.0 copy-start.1

commit v2 on v1

--- a/solution.py
+++ b/solution.py
@@ -43,14 +43,21 @@
 
 def body(
     n_dp,
-    lens, tok, cot, g1, s1, ob, g2, s2, db, bias, wq_in, wo_in, wu_in, wd_in,
-    lo, tg, gsum, small, wd_full,
+    lens, tok_in, cot_in, g1, s1, ob, g2, s2, db, ub_in, qvb_in, wq_in, wo_in, wu_in, wd_in,
+    lo_out, tg_out, gsum, small, wd_full,
+    tok, cot, lo, tg, bias, vecs, qvb,
     wq, wo, wu, wdbuf, biasg, n1, q, k, v, p, dsb, att, mixed, mg, n2, mgl, act, gp, mask,
     csend, crecv, xsend, keep, xrecv, yrecv, zrecv, fin, orecv, srecv,
-    own_sem, ag_s, ag_r, b_s, b_r, wd_sem, c_s, c_r, credit, x_s, x_r, y_s, y_r, z_s, z_r,
+    io_sem, own_sem, own_s, own_r, far_r, ag_s, ag_r, b_s, b_r, wd_sem, c_s, c_r, credit, x_s, x_r, y_s, y_r, z_s, z_r,
     a_s, a_r, e_s, e_r, l_s, o_s, o_r, v_s, v_r,
 ):
     rows, d = tok.shape
+    c_tok = pltpu.make_async_copy(tok_in, tok, io_sem.at[0])
+    c_cot = pltpu.make_async_copy(cot_in, cot, io_sem.at[1])
+    c_lo = pltpu.make_async_copy(lo, lo_out, io_sem.at[2])
+    c_tg = pltpu.make_async_copy(tg, tg_out, io_sem.at[3])
+    c_tok.start()
+    c_cot.start()
     hw = wo_in.shape[0]
     ff = wu_in.shape[1]
     half_w = 2 * hw
@@ -80,123 +87,150 @@
     peers_dp = [yn] + z_devs + o_devs
     peers = [(dp, sib), (dp, xn), (dp, m_sx)] + [(e, mp) for e in peers_dp]
 
+    bias[...] = jnp.zeros_like(bias)
+    bias[0:1, :] = ub_in[...].reshape(1, d)
+    bias[1:3, 0:hw] = qvb_in[...]
+    for n, ref in enumerate((g1, s1, ob, g2, s2, db)):
+        vecs[n:n + 1, :] = ref[...].reshape(1, d)
+    g1, s1, ob, g2, s2, db = (vecs.at[pl.ds(n, 1)] for n in range(6))
     barrier = pltpu.get_barrier_semaphore()
     for dev in peers:
         pl.semaphore_signal(barrier, inc=1, device_id=dev, device_id_type=MESH)
     pl.semaphore_wait(barrier, len(peers))
 
-    quarter = [hw // 4, hw // 4, d // 4, ff // 4]
-
-    def own(t, r0, n):
-        if t == 0:
-            return wq_in.at[:, pl.ds(r0, n), :]
-        return (wo_in, wu_in, wd_in)[t - 1].at[pl.ds(r0, n), :]
-
-    def full(t, m, r0, n):
-        if t == 0:
-            return wq.at[:, pl.ds(pl.multiple_of(m * hw + r0, 16), n), :]
-        if t == 1:
-            return wo.at[pl.ds(pl.multiple_of(m * hw + r0, 16), n), :]
-        return (wu, wd_full)[t - 2].at[m, pl.ds(r0, n), :]
+    n_units = 12
+    quarter = hw // 4
+
+    def own(u, r0, n):
+        if u < 3:
+            return wq_in.at[u, pl.ds(r0, n), :]
+        if u == 3:
+            return wo_in.at[pl.ds(r0, n), :]
+        return (wu_in if u < 8 else wd_in).at[pl.ds((u % 4) * hw + r0, n), :]
+
+    def full(u, m, r0, n):
+        if u < 4:
+            return (wq.at[u] if u < 3 else wo).at[pl.ds(pl.multiple_of(m * hw + r0, 16), n), :]
+        return (wu if u < 8 else wd_full).at[m, pl.ds((u % 4) * hw + r0, n), :]
 
     q_own = y + 2 * z1
     q_y, q_z, q_d = (1 - y) + 2 * z1, y + 2 * (1 - z1), (1 - y) + 2 * (1 - z1)
 
-    def reg(t, m, qq, part=None):
-        n = quarter[t]
-        r0 = pl.multiple_of(qq * n, 16)
-        if part is None:
-            return full(t, m, r0, n)
+    def start_of(qq):
+        return pl.multiple_of(qq * quarter, 16)
+
+    def reg(u, m, qq):
+        return full(u, m, start_of(qq), quarter)
+
+    def shard_in(t):
+        return (wq_in, wo_in, wu_in, wd_in)[t]
+
+    def whole(t, m):
         if t == 0:
-            ref = wq.at[pl.ds(0, 1)] if part == "y" else wq.at[pl.ds(1, 2)]
-            return ref.at[:, pl.ds(pl.multiple_of(m * hw + r0, 16), n), :]
+            return wq.at[:, pl.ds(pl.multiple_of(m * hw, 16), hw), :]
         if t == 1:
-            return full(t, m, r0, n)
-        return full(t, m, r0 + (0 if part == "y" else n // 2), n // 2)
-
-    def whole(t, m):
-        return full(t, m, 0, 4 * quarter[t])
+            return wo.at[pl.ds(pl.multiple_of(m * hw, 16), hw), :]
+        return (wu, wd_full)[t - 2].at[m]
+
+    def tensor_of(u):
+        return 0 if u < 3 else 1 if u == 3 else 2 if u < 8 else 3
+
+    def kind(u):
+        return "x" if u < 4 else "yz"[u % 2]
 
     dev_s, dev_x, dev_y, dev_z = (dp, sib), (dp, xn), (yn, mp), (zn, mp)
 
     def c_own(t):
-        return pltpu.make_async_copy(own(t, 0, 4 * quarter[t]), whole(t, mp), own_sem.at[t])
+        return pltpu.make_async_copy(shard_in(t), whole(t, mp), own_sem.at[t])
 
     def d_own(t):
-        return rc(own(t, 0, 4 * quarter[t]), whole(t, mp), ag_s.at[t, 0], ag_r.at[t, 0], dev_s)
-
-    def d_x(t):
-        n = quarter[t]
-        return rc(own(t, pl.multiple_of(q_own * n, 16), n), reg(t, mp, q_own), ag_s.at[t, 1], ag_r.at[t, 1], dev_x)
-
-    def fwd(t, qq, part, si, ri, dev):
-        r = reg(t, m_x, qq, part)
-        return rc(r, r, ag_s.at[t, si], ag_r.at[t, ri], dev)
-
-    def d_y(t):
-        return fwd(t, q_own, None, 2, 2, dev_y)
-
-    def d_z(t):
-        return fwd(t, q_own, None, 3, 3, dev_z)
-
-    def d_s(t, qq, si):
-        return fwd(t, qq, None, si, 6, dev_s)
-
-    def d_dz(t):
-        return fwd(t, q_y, "z", 6, 4, dev_z)
-
-    def d_dy(t):
-        return fwd(t, q_z, "y", 8, 5, dev_y)
+        return rc(shard_in(t), whole(t, mp), own_s.at[t], own_r.at[t], dev_s)
+
+    def d_x(u):
+        return rc(own(u, start_of(q_own), quarter), reg(u, mp, q_own), ag_s.at[u, 0], ag_r.at[u, 0], dev_x)
+
+    def d_xd(u):
+        return rc(own(u, start_of(q_d), quarter), reg(u, mp, q_d), ag_s.at[u, 1], ag_r.at[u, 1], dev_x)
+
+    def fwd(u, qq, si, rs, dev):
+        r = reg(u, m_x, qq)
+        return rc(r, r, ag_s.at[u, si], rs, dev)
+
+    def d_y(u):
+        return fwd(u, q_own, 2, ag_r.at[u, 2], dev_y)
+
+    def d_z(u):
+        return fwd(u, q_own, 3, ag_r.at[u, 3], dev_z)
+
+    def d_s(u, qq, si):
+        return fwd(u, qq, si, far_r.at[tensor_of(u)], dev_s)
+
+    def d_dg(u):
+        if kind(u) == "y":
+            return fwd(u, q_z, 1, ag_r.at[u, 1], dev_y)
+        return fwd(u, q_y, 1, ag_r.at[u, 1], dev_z)
 
     def arrive(region, sem, dev):
         rc(region, region, ag_s.at[0, 0], sem, dev).wait_recv()
 
-    def f1(t):
-        arrive(reg(t, m_x, q_own), ag_r.at[t, 1], dev_x)
-        d_y(t).start()
-        d_z(t).start()
-        d_s(t, q_own, 4).start()
-
-    def f2(t):
-        arrive(reg(t, m_x, q_y), ag_r.at[t, 2], dev_y)
-        if t != 1:
-            d_dz(t).start()
-        d_s(t, q_y, 5).start()
-        arrive(reg(t, m_x, q_z), ag_r.at[t, 3], dev_z)
-        d_dy(t).start()
-        d_s(t, q_z, 7).start()
-
-    def f3(t):
-        if t != 1:
-            arrive(reg(t, m_x, q_d, "z"), ag_r.at[t, 4], dev_z)
-        arrive(reg(t, m_x, q_d, "y"), ag_r.at[t, 5], dev_y)
-        d_s(t, q_d, 9).start()
+    def f1(u):
+        arrive(reg(u, m_x, q_own), ag_r.at[u, 0], dev_x)
+        d_y(u).start()
+        d_z(u).start()
+        d_s(u, q_own, 4).start()
+
+    def f2(u):
+        arrive(reg(u, m_x, q_y), ag_r.at[u, 2], dev_y)
+        arrive(reg(u, m_x, q_z), ag_r.at[u, 3], dev_z)
+        if kind(u) != "x":
+            d_dg(u).start()
+        d_s(u, q_y, 5).start()
+        d_s(u, q_z, 6).start()
+
+    def f3(u):
+        arrive(reg(u, m_x, q_d), ag_r.at[u, 1], {"x": dev_x, "y": dev_y, "z": dev_z}[kind(u)])
+        d_s(u, q_d, 7).start()
+
+    def do(*todo):
+        for step, u in todo:
+            (f1, f2, f3)[step - 1](u)
 
     def near(t):
-        c_own(t).wait()
-        arrive(whole(t, sib), ag_r.at[t, 0], dev_s)
+        if t < 3:
+            c_own(t).wait()
+        arrive(whole(t, sib), own_r.at[t], dev_s)
 
     def far(t):
-        arrive(whole(t, m_sx), ag_r.at[t, 6], dev_s)
-
-    def sent(t):
-        for cp in (d_own(t), d_x(t), d_y(t), d_z(t), d_s(t, q_own, 4), d_s(t, q_y, 5), d_s(t, q_z, 7),
-                   d_dy(t), d_s(t, q_d, 9)):
-            cp.wait_send()
-        if t != 1:
-            d_dz(t).wait_send()
+        arrive(whole(t, m_sx), far_r.at[t], dev_s)
+
+    def sent():
+        for t in range(4):
+            d_own(t).wait_send()
+        for u in range(n_units):
+            for cp in (d_x(u), d_xd(u) if kind(u) == "x" else d_dg(u), d_y(u), d_z(u), d_s(u, q_own, 4),
+                       d_s(u, q_y, 5), d_s(u, q_z, 6), d_s(u, q_d, 7)):
+                cp.wait_send()
 
     def d_bias(i):
         dev = [sib, xn, m_sx][i]
         return rc(bias, biasg.at[mp], b_s.at[i], b_r.at[i], (dp, dev))
 
-    for t in range(4):
-        d_x(t).start()
+    for u in range(3):
+        d_x(u).start()
+    d_own(0).start()
+    c_own(0).start()
+    for i in range(3):
+        d_bias(i).start()
+    for u in range(3):
+        d_xd(u).start()
+    for u in range(3, n_units):
+        d_x(u).start()
+        if kind(u) == "x":
+            d_xd(u).start()
+    for t in range(1, 4):
         d_own(t).start()
-        c_own(t).start()
-        if t == 0:
-            for i in range(3):
-                d_bias(i).start()
+        if t < 3:
+            c_own(t).start()
 
     def rows_of(ref, r0, n):
         return ref.at[pl.ds(pl.multiple_of(r0, 16), n), :]
@@ -313,20 +347,23 @@
 
     stages = [st_y, st_z, st_a] + ([st_o] if n_out > 1 else []) + [st_b, st_e]
 
+    gap = 2
+
     def tick(t):
         for s in reversed(range(len(stages))):
-            u = t - s
+            u = t - gap * s
 
             @pl.when(jnp.logical_and(u >= 0, u < n_chunks))
             def _(s=s, u=u):
                 stages[s](u)
 
-    def d_c(slot):
-        return rc(csend.at[slot], crecv.at[slot], c_s.at[slot], c_r.at[slot], dev_s)
+    def d_c(slot, r0, n, j):
+        part = pl.ds(pl.multiple_of(r0, 16), n)
+        return rc(csend.at[slot, part, :], crecv.at[slot, part, :], c_s.at[slot, j], c_r.at[slot, j], dev_s)
 
     def m_of(i):
-        mx = jnp.where(i % 2 == 0, 1 - x, x)
-        mc = jnp.where(i < 2, 1 - c, c)
+        mx = jnp.where(i < 2, 1 - x, x)
+        mc = jnp.where(i % 2 == 0, 1 - c, c)
         return 2 * mx + mc
 
     small[...] = jnp.zeros_like(small)
@@ -338,8 +375,8 @@
         xc = xv - jnp.mean(xv, axis=-1, keepdims=True)
         inv = lax.rsqrt(jnp.mean(xc * xc, axis=-1, keepdims=True) + EPS)
         n1[r, :] = (xc * inv * g1[...] + s1[...]).astype(BF16)
-        small[5:6, :] += jnp.sum(cot[r, :].astype(F32), axis=0, keepdims=True)
-
+
+    c_tok.wait()
     loop(rows // rb, ln1)
 
     n_seg = lens.shape[1]
@@ -357,8 +394,11 @@
     biasg[mp] = bias[...]
     for i in range(3):
         d_bias(i).wait()
-    bias_sum = biasg[0, 1:3, :] + biasg[1, 1:3, :] + biasg[2, 1:3, :] + biasg[3, 1:3, :]
-    small[14:16, :] = bias_sum
+    tot = biasg[0]
+    for m in range(1, 4):
+        tot = tot + pltpu.roll(biasg[m], hw * m, 1)
+    qvb[...] = tot
+    do((1, 0))
 
     scale = 1.0 / math.sqrt(HD)
     n_pairs = d // (2 * HD)
@@ -393,9 +433,9 @@
             for cc, ref in enumerate((q, k, v)):
                 val = nt(n1[...], wq[cc, w_rows, :])
                 if cc == 0:
-                    val = val + small[14:15, w_lanes]
+                    val = val + qvb[1:2, w_lanes]
                 if cc == 2:
-                    val = val + small[15:16, w_lanes]
+                    val = val + qvb[2:3, w_lanes]
                 val = val.astype(BF16)
                 if cc == 0:
                     val = val * jnp.asarray(scale, BF16)
@@ -415,25 +455,31 @@
             o2 = jnp.where(low_half, outs[0], outs[1]) * kept[r * ab:(r + 1) * ab]
             att[rs, lanes] = o2.astype(BF16)
 
-        for at, todo in enumerate(AG_PLAN):
-            @pl.when(i == at)
-            def _(todo=todo):
-                for fn, t in todo:
-                    (f1, f2, f3)[fn - 1](t)
-
-    AG_PLAN = [
-        [(1, 0)],
-        [(2, 0), (1, 1)],
-        [(3, 0), (2, 1), (1, 2)],
-        [(3, 1), (2, 2), (1, 3)],
-        [(3, 2), (2, 3)],
-        [(3, 3)],
-    ]
+            for at, todo in AG_PLAN.items():
+                if at % 2 == r:
+                    @pl.when(i == at // 2)
+                    def _(todo=todo):
+                        do(*todo)
+
+    AG_PLAN = {
+        0: [(1, 1), (1, 2)],
+        1: [(2, 0)],
+        2: [(2, 1), (3, 0)],
+        4: [(2, 2), (3, 1)],
+        5: [(3, 2)],
+        6: [(1, 3), (3, 3), (2, 3)],
+        7: [(1, 4)],
+        8: [(1, 5)],
+        9: [(2, 4)],
+        10: [(1, 6)],
+        11: [(1, 7), (2, 5)],
+    }
     loop(n_pairs, attn_fwd)
 
     near(1)
     far(1)
     mixed[...] = nn(att[...], wo[...])
+    do((1, 8), (2, 6), (3, 4))
 
     def ln2(i):
         r = pl.ds(pl.multiple_of(i * rb, rb), rb)
@@ -445,55 +491,55 @@
         n2[r, :] = (xc * inv * g2[...] + s2[...]).astype(BF16)
 
     loop(rows // rb, ln2)
+    do((2, 7), (3, 5), (1, 9), (3, 6), (1, 10), (3, 7))
 
     tile = 256
 
     def emit_block(g, i, make):
+        slot, mine = i // 2, i % 2 == 1
+        n_parts = d // tile
         if g > 0:
-            @pl.when(i < 2)
+            @pl.when(jnp.logical_not(mine))
             def _():
-                pl.semaphore_wait(credit.at[i], 1)
-                d_c(i).wait_send()
-
-        @pl.when(i >= 2)
-        def _():
-            d_c(i - 2).wait_recv()
+                pl.semaphore_wait(credit.at[slot], 1)
+                for r in range(n_parts):
+                    d_c(slot, r * tile, tile, r).wait_send()
 
         def part(r):
             rr = pl.ds(pl.multiple_of(r * tile, tile), tile)
             res = make(r)
 
-            @pl.when(i < 2)
+            @pl.when(jnp.logical_not(mine))
             def _():
-                csend[i, rr, :] = res.astype(BF16)
-
-            @pl.when(i >= 2)
+                csend[slot, rr, :] = res.astype(BF16)
+                d_c(slot, r * tile, tile, r).start()
+
+            @pl.when(mine)
             def _():
-                tot = (res + crecv[i - 2, rr, :].astype(F32)).astype(BF16)
+                d_c(slot, r * tile, tile, r).wait_recv()
+                tot = (res + crecv[slot, rr, :].astype(F32)).astype(BF16)
                 out = pl.ds(pl.multiple_of(g * d + r * tile, tile), tile)
 
-                @pl.when(i == 2)
+                @pl.when(slot == 0)
                 def _():
                     xsend[out, :] = tot
                     for cc in range(tile // CHUNK):
                         d_xs(g * per_group + r * (tile // CHUNK) + cc).start()
 
-                @pl.when(i == 3)
+                @pl.when(slot == 1)
                 def _():
                     keep[out, :] = tot
 
-        loop(d // tile, part)
-
-        @pl.when(i < 2)
-        def _():
-            d_c(i).start()
-
-        @pl.when(i >= 2)
-        def _():
-            pl.semaphore_signal(credit.at[i - 2], inc=1, device_id=dev_s, device_id_type=MESH)
+        loop(n_parts, part)
+
+        @pl.when(mine)
+        def _():
+            pl.semaphore_signal(credit.at[slot], inc=1, device_id=dev_s, device_id_type=MESH)
 
     near(2)
     far(2)
+
+    c_cot.wait()
 
     def ffn1(i):
         m = m_of(i)
@@ -513,6 +559,11 @@
 
         emit_block(0, i, make)
 
+        for at, todo in enumerate(([(1, 11), (2, 8), (2, 9), (3, 8)], [(2, 10), (3, 9), (2, 11)], [(3, 10), (3, 11)])):
+            @pl.when(i == at)
+            def _(todo=todo):
+                do(*todo)
+
     loop(4, ffn1)
 
     near(3)
@@ -521,7 +572,16 @@
     def c_wd(i):
         return pltpu.make_async_copy(wd_full.at[m_of(i)], wdbuf.at[i % 2], wd_sem.at[i % 2])
 
-    c_wd(0).start()
+    def start_wd(i):
+        @pl.when(i < 3)
+        def _():
+            c_wd(i).start()
+
+        @pl.when(i == 3)
+        def _():
+            pltpu.make_async_copy(wd_in, wdbuf.at[i % 2], wd_sem.at[i % 2]).start()
+
+    start_wd(0)
     mg[...] = jnp.zeros_like(mg)
 
     def ffn2(i):
@@ -530,7 +590,7 @@
 
         @pl.when(i < 3)
         def _():
-            c_wd(i + 1).start()
+            start_wd(i + 1)
 
         s = i % 2
 
@@ -547,6 +607,7 @@
             return tn(n2[:, rl], gp[m])
 
         emit_block(1, i, make)
+        tick(jnp.where(i == 0, 0, i + 1))
 
         def back(n):
             nl = pl.ds(pl.multiple_of(n * tile, tile), tile)
@@ -554,9 +615,13 @@
             lo[:, nl] += nn(act[m], wdbuf[s, :, nl])
 
         loop(d // tile, back)
-        tick(i)
+
+        @pl.when(i == 0)
+        def _():
+            tick(1)
 
     loop(4, ffn2)
+    c_lo.start()
 
     def ln2b(i):
         r = pl.ds(pl.multiple_of(i * rb, rb), rb)
@@ -574,6 +639,7 @@
         mg[r, :] = val
         mgl[r, :] = val.astype(BF16)
         small[4:5, :] += jnp.sum(val, axis=0, keepdims=True)
+        small[5:6, :] += jnp.sum(cot[r, :].astype(F32), axis=0, keepdims=True)
 
     loop(rows // rb, ln2b)
 
@@ -584,7 +650,7 @@
         da[:, nl] = (nt(mgl[...], wo[nl, :]).astype(BF16).astype(F32) * kept).astype(BF16)
 
     loop(d // tile, dab)
-    tick(4)
+    tick(5)
 
     def attn_bwd(i):
         xh, pair, lanes = lanes_of((i + per_half) % n_pairs)
@@ -618,14 +684,15 @@
             a = i // per_half
             wl = pl.ds(pl.multiple_of(xh * half_w, 128), half_w)
             pl.semaphore_wait(credit.at[a], 1)
-            d_c(a).wait_send()
+            for r in range(d // tile):
+                d_c(a, r * tile, tile, r).wait_send()
             for j, (ref, other) in enumerate(((att, mgl), (q, n1), (k, n1), (v, n1))):
                 act[pl.ds(0, 2), pl.ds(0, hw), :] = tn(ref[:, wl], other[...]).astype(BF16).reshape(2, hw, d)
                 csend[a, j * hw:(j + 1) * hw, :] = act[1 - c, 0:hw, :]
+                d_c(a, j * hw, hw, j).start()
                 gp[0 if j < 2 else 1, (j % 2) * hw:(j % 2 + 1) * hw, :] = act[c, 0:hw, :]
-            d_c(a).start()
-            d_c(a).wait_recv()
             for j in range(4):
+                d_c(a, j * hw, hw, j).wait_recv()
                 tot = (gp[0 if j < 2 else 1, (j % 2) * hw:(j % 2 + 1) * hw, :].astype(F32)
                        + crecv[a, j * hw:(j + 1) * hw, :].astype(F32)).astype(BF16)
 
@@ -642,7 +709,7 @@
                 for cc in range(per_group):
                     d_xs(2 * per_group + cc).start()
 
-        tick(5 + i)
+        tick(6 + i)
 
     loop(n_pairs, attn_bwd)
 
@@ -667,13 +734,14 @@
         ) * inv
 
     loop(rows // rb, ln1b)
+    c_tg.start()
 
     v_devs = [(dp, sib), (dp, xn)] + [(flip(dp, b), mp) for b in bits]
 
     def d_v(s):
         return rc(small, srecv.at[s], v_s.at[s], v_r.at[s], v_devs[s])
 
-    first = 5 + n_pairs
+    first = 6 + n_pairs
 
     def tail(i):
         for s in range(len(v_devs) + 1):
@@ -687,11 +755,13 @@
 
         tick(first + i)
 
-    loop(max(n_chunks + len(stages) - 1 - first, len(v_devs) + 1), tail)
+    loop(max(n_chunks + gap * (len(stages) - 1) - first, len(v_devs) + 1), tail)
     for slot in range(2):
-        d_c(slot).wait_send()
-    for t in range(4):
-        sent(t)
+        for j in range(4):
+            d_c(slot, j * hw, hw, j).wait_send()
+    sent()
+    c_lo.wait()
+    c_tg.wait()
 
 
 def layer(n_dp, tokens, lens, g1, s1, wqkv, qvb, wo, ob, g2, s2, wu, ub, wd, db, cot):
@@ -705,12 +775,6 @@
     nc = 3 * d // CHUNK
     n_small = 2 + n_dp.bit_length() - 1
     heads = d // HD
-    vec = lambda a: a.reshape(1, d)
-    lane = jnp.arange(d, dtype=jnp.int32)[None, :]
-    wide = jnp.concatenate([qvb] * n_mp, axis=1)
-    bias = jnp.concatenate(
-        [ub.reshape(1, d), jnp.where(lane // hw == mp, wide, 0.0), jnp.zeros((5, d), F32)], axis=0
-    )
     wqt = jnp.swapaxes(wqkv, 1, 2)
     vm = pl.BlockSpec(memory_space=pltpu.VMEM)
     hbm = pl.BlockSpec(memory_space=pl.ANY)
@@ -725,9 +789,11 @@
         out_shape=(
             S((rows, d), F32), S((rows, d), F32), S((3 * d, d), BF16), S((16, d), F32), S((n_mp, ff, d), BF16),
         ),
-        in_specs=[sm] + [vm] * 9 + [hbm] * 4,
-        out_specs=(vm, vm, hbm, vm, hbm),
+        in_specs=[sm] + [hbm] * 2 + [vm] * 8 + [hbm] * 4,
+        out_specs=(hbm, hbm, hbm, vm, hbm),
         scratch_shapes=[
+            V((rows, d), BF16), V((rows, d), BF16), V((rows, d), F32), V((rows, d), F32), V((8, d), F32), V((8, d), F32),
+            V((8, d), F32),
             V((3, d, d), BF16), V((d, d), BF16), V((n_mp, d, ff), BF16), V((2, ff, d), BF16), V((n_mp, 8, d), F32),
             V((rows, d), BF16), V((rows, d), BF16), V((rows, d), BF16), V((rows, d), BF16),
             V((heads, rows, rows), BF16), V((rows, rows), BF16), V((rows, d), BF16),
@@ -736,7 +802,8 @@
             V((2, d, d), BF16), V((2, d, d), BF16), V((3 * d, d), BF16), V((3 * d, d), BF16), V((3 * d, d), BF16),
             V((nc * CHUNK // 2, d), BF16), V((nzr * piece, d), BF16), V((nc * piece, d), BF16),
             V((nor * piece, d), BF16), V((n_small, 16, d), F32),
-            dma((4,)), dma((4, 10)), dma((4, 7)), dma((3,)), dma((3,)), dma((2,)), dma((2,)), dma((2,)),
+            dma((4,)), dma((4,)), dma((4,)), dma((4,)), dma((4,)), dma((12, 8)), dma((12, 4)), dma((3,)), dma((3,)),
+            dma((2,)), dma((2, 4)), dma((2, 4)),
             pltpu.SemaphoreType.REGULAR((2,)), dma((nc,)), dma((nc,)), dma((nc,)), dma((nc,)),
             dma((nzr,)), dma((nzr,)), dma((nzr,)), dma((nzr,)), dma((nc,)), dma((nc,)), dma((nc,)),
             dma((nor,)), dma((nor,)), dma((n_small,)), dma((n_small,)),
@@ -745,15 +812,59 @@
             collective_id=0, has_side_effects=True, vmem_limit_bytes=67043328
         ),
         name="layer",
-    )(lens, tokens, cot, vec(g1), vec(s1), vec(ob), vec(g2), vec(s2), vec(db), bias, wqt, wo, wu, wd)
-
-    f = lambda a: a.astype(F32)
-    dqkv = f(jnp.swapaxes(gsum[2 * d + hw:].reshape(3, hw, d), 1, 2))
-    qv = lax.dynamic_slice(small, (6, mp * hw), (2, hw))
-    upb = lax.dynamic_slice(small, (8 + mp, 0), (1, d)).reshape(d)
+    )(lens, tokens, cot, g1, s1, ob, g2, s2, db, ub, qvb, wqt, wo, wu, wd)
+
+    steps = 8
+    part, rpart = d // steps, rows // steps
+    opart = hw // 2
+
+    def finish(down, up, rest, lo_ref, tg_ref, sm_ref, o_down, o_up, o_out, o_qkv, o_lo, o_tg,
+               o_g1, o_s1, o_g2, o_s2, o_ob, o_db, o_qv, o_ub):
+        i = pl.program_id(0)
+        o_down[...] = down[...].astype(F32)
+        o_up[...] = up[...].astype(F32)
+        o_lo[...] = lo_ref[...]
+        o_tg[...] = tg_ref[...]
+
+        @pl.when(i < 2)
+        def _():
+            o_out[...] = rest[...].astype(F32)
+
+        @pl.when(i >= 2)
+        def _():
+            o_qkv[0] = rest[...].astype(F32)
+
+        @pl.when(i == 0)
+        def _():
+            for n, ref in enumerate((o_g1, o_s1, o_g2, o_s2, o_ob, o_db)):
+                ref[...] = sm_ref[n:n + 1, :].reshape(d)
+            me = lax.axis_index("mp")
+            o_ub[...] = sm_ref[pl.ds(8 + me, 1), :].reshape(d)
+            acc = jnp.zeros((2, hw), F32)
+            for m in range(n_mp):
+                acc = jnp.where(me == m, sm_ref[6:8, m * hw:(m + 1) * hw], acc)
+            o_qv[...] = acc
+
+    blk = lambda off: pl.BlockSpec((part, d), lambda i: (i + off, 0))
+    row = pl.BlockSpec((rpart, d), lambda i: (i, 0))
+    one = pl.BlockSpec((d,), lambda i: (0,))
+    dwn, up_g, out_g, qkv_g, lo, tg, o_g1, o_s1, o_g2, o_s2, o_ob, o_db, o_qv, o_ub = pl.pallas_call(
+        finish,
+        grid=(steps,),
+        out_shape=(
+            S((ff, d), F32), S((d, ff), F32), S((hw, d), F32), S((3, hw, d), F32), S((rows, d), F32), S((rows, d), F32),
+            S((d,), F32), S((d,), F32), S((d,), F32), S((d,), F32), S((d,), F32), S((d,), F32), S((2, hw), F32), S((d,), F32),
+        ),
+        in_specs=[blk(0), blk(steps), blk(2 * steps), row, row, pl.BlockSpec((16, d), lambda i: (0, 0))],
+        out_specs=(
+            blk(0), blk(0), pl.BlockSpec((opart, d), lambda i: (jnp.minimum(i, 1), 0)),
+            pl.BlockSpec((1, opart, d), lambda i: (jnp.maximum(i - 2, 0) // 2, jnp.maximum(i - 2, 0) % 2, 0)), row, row,
+            one, one, one, one, one, one, pl.BlockSpec((2, hw), lambda i: (0, 0)), one,
+        ),
+        name="finish",
+    )(gsum, gsum, gsum, lo, tg, small)
     return (
-        lo, tg, small[0], small[1], dqkv, qv, f(gsum[2 * d:2 * d + hw]), small[4], small[2], small[3],
-        f(gsum[d:2 * d]), upb, f(gsum[:d]), small[5],
+        lo, tg, o_g1, o_s1, jnp.swapaxes(qkv_g, 1, 2), o_qv, out_g, o_ob, o_g2, o_s2, up_g, o_ub, dwn, o_db,
     )
 
 

time: 221 us -> 193 us (0.87)
  local copies, waits for them, and re-layouts: 15.9 us -> 0 us
  other arithmetic: 7.3 us -> 0 us
  Pallas kernels: 197 us -> 191 us
    pallas_call x1, Pallas kernels: 197 us -> 182 us  [layer(): pl.pallas_call(functools.partial(body, n_dp), out_shape=(S((rows, d), F32...]
    pallas_call x0 -> x1, Pallas kernels: none -> 9.62 us  [layer(): pl.pallas_call(finish, grid=(steps,), out_shape=(S((ff, d), F32), S((d, f...]
    reshape x7 -> x0, local copies, waits for them, and re-layouts: 8.29 us -> none  [the longest x6 7.6 us: layer(): vec = lambda a: a.reshape(1, d)]
    convert_element_type x3 -> x0, other arithmetic: 5.71 us -> none  [layer(): f = lambda a: a.astype(F32)]
    unnamed x8 -> x0, local copies, waits for them, and re-layouts: 3.12 us -> none
    slice x2 -> x0, local copies, waits for them, and re-layouts: 3.01 us -> none  [the longest x1 1.63 us: layer(): small[5]]
where the time goes in v2:
time: 193 us; the launch traced here: 192 us
  Pallas kernels  191 us (99%)
    pallas_call x1, Pallas kernels, layer(): pl.pallas_call(functools.partial(body, n_dp), out_shape=(S((rows, d), F32...  182 us
    pallas_call x1, Pallas kernels, layer(): pl.pallas_call(finish, grid=(steps,), out_shape=(S((ff, d), F32), S((d, f...  9.62 us

profile of v2, /device:TPU:0, one launch (start us, length us, event | category | flops | bytes accessed | tf_op | source)
XLA Modules:
  0.0 192.1 jit_solution(5992695270888892462)
XLA Ops:
  0.7 181.9 %layer.1 = (f32[512,768]{1,0:T(8,128)}, f32[512,768]{1,0:T(8,128)}, bf16[2304,768]{1,0:T(8,128)(2,1)}, f32[16,768]{1,0:T(8,128)}, bf16[4,768,768]{2,1,0:T(8,128)(2,1)}) custom-call(s32[4,8]{1,0:T(4,128)} %lens.1, bf16[512,768]{1,0:T(8,128)(2,1)} %tok_in.1, bf16[512,768]{1,0:T(8,128)(2,1)} %cot_in.1, f32[768]{0:T(1024)} %g1.1, f32[768]{0:T(1024)} %s1_.1, ...), custom_call_target="tpu_custom_call" | custom-call | tf_op jit(solution)/shard_map/layer/pallas_call | solution.py:787
  182.5 9.6 %finish.1 = (f32[768,768]{1,0:T(8,128)}, f32[768,768]{1,0:T(8,128)}, f32[192,768]{1,0:T(8,128)}, f32[3,192,768]{2,1,0:T(8,128)}, f32[512,768]{1,0:T(8,128)}, /*i...) custom-call(bf16[2304,768]{1,0:T(8,128)(2,1)} %get-tuple-element.32., ...), custom_call_target="tpu_custom_call" | custom-call | tf_op jit(solution)/shard_map/finish/pallas_call | solution.py:851

commit v3 on v2

--- a/solution.py
+++ b/solution.py
@@ -136,7 +136,7 @@
         return 0 if u < 3 else 1 if u == 3 else 2 if u < 8 else 3
 
     def kind(u):
-        return "x" if u < 4 else "yz"[u % 2]
+        return "xyz"[u % 3]
 
     dev_s, dev_x, dev_y, dev_z = (dp, sib), (dp, xn), (yn, mp), (zn, mp)
 
@@ -221,12 +221,11 @@
     c_own(0).start()
     for i in range(3):
         d_bias(i).start()
-    for u in range(3):
-        d_xd(u).start()
+    d_xd(0).start()
     for u in range(3, n_units):
         d_x(u).start()
-        if kind(u) == "x":
-            d_xd(u).start()
+        if u % 3 == 2:
+            d_xd(u - 2).start()
     for t in range(1, 4):
         d_own(t).start()
         if t < 3:
@@ -398,7 +397,6 @@
     for m in range(1, 4):
         tot = tot + pltpu.roll(biasg[m], hw * m, 1)
     qvb[...] = tot
-    do((1, 0))
 
     scale = 1.0 / math.sqrt(HD)
     n_pairs = d // (2 * HD)
@@ -425,6 +423,7 @@
         @pl.when(i == per_half)
         def _():
             far(0)
+            do((1, 5))
 
         @pl.when(i % per_half == 0)
         def _():
@@ -462,24 +461,22 @@
                         do(*todo)
 
     AG_PLAN = {
-        0: [(1, 1), (1, 2)],
-        1: [(2, 0)],
-        2: [(2, 1), (3, 0)],
-        4: [(2, 2), (3, 1)],
-        5: [(3, 2)],
-        6: [(1, 3), (3, 3), (2, 3)],
-        7: [(1, 4)],
-        8: [(1, 5)],
-        9: [(2, 4)],
-        10: [(1, 6)],
-        11: [(1, 7), (2, 5)],
+        0: [(1, 0)],
+        1: [(1, 1)],
+        3: [(2, 0), (1, 2)],
+        5: [(2, 1), (3, 0), (2, 2), (1, 3), (3, 1), (3, 2), (1, 4)],
+        6: [(2, 3), (2, 4), (3, 3)],
+        7: [(1, 6), (2, 5)],
+        9: [(1, 7), (3, 4)],
+        10: [(3, 5)],
+        11: [(1, 8), (2, 6)],
     }
     loop(n_pairs, attn_fwd)
 
     near(1)
     far(1)
     mixed[...] = nn(att[...], wo[...])
-    do((1, 8), (2, 6), (3, 4))
+    do((2, 7), (3, 6))
 
     def ln2(i):
         r = pl.ds(pl.multiple_of(i * rb, rb), rb)
@@ -491,7 +488,7 @@
         n2[r, :] = (xc * inv * g2[...] + s2[...]).astype(BF16)
 
     loop(rows // rb, ln2)
-    do((2, 7), (3, 5), (1, 9), (3, 6), (1, 10), (3, 7))
+    do((1, 9), (2, 8), (3, 7), (1, 10))
 
     tile = 256
 
@@ -559,7 +556,7 @@
 
         emit_block(0, i, make)
 
-        for at, todo in enumerate(([(1, 11), (2, 8), (2, 9), (3, 8)], [(2, 10), (3, 9), (2, 11)], [(3, 10), (3, 11)])):
+        for at, todo in enumerate(([(1, 11), (2, 9), (3, 8), (2, 10), (3, 9)], [(2, 11), (3, 10)], [(3, 11)])):
             @pl.when(i == at)
             def _(todo=todo):
                 do(*todo)
@@ -607,7 +604,7 @@
             return tn(n2[:, rl], gp[m])
 
         emit_block(1, i, make)
-        tick(jnp.where(i == 0, 0, i + 1))
+        tick(jnp.where(i < 2, 2 * i, i + 2))
 
         def back(n):
             nl = pl.ds(pl.multiple_of(n * tile, tile), tile)
@@ -616,9 +613,9 @@
 
         loop(d // tile, back)
 
-        @pl.when(i == 0)
-        def _():
-            tick(1)
+        @pl.when(i < 2)
+        def _():
+            tick(2 * i + 1)
 
     loop(4, ffn2)
     c_lo.start()
@@ -650,7 +647,7 @@
         da[:, nl] = (nt(mgl[...], wo[nl, :]).astype(BF16).astype(F32) * kept).astype(BF16)
 
     loop(d // tile, dab)
-    tick(5)
+    tick(6)
 
     def attn_bwd(i):
         xh, pair, lanes = lanes_of((i + per_half) % n_pairs)
@@ -709,7 +706,7 @@
                 for cc in range(per_group):
                     d_xs(2 * per_group + cc).start()
 
-        tick(6 + i)
+        tick(7 + i)
 
     loop(n_pairs, attn_bwd)
 
@@ -741,7 +738,7 @@
     def d_v(s):
         return rc(small, srecv.at[s], v_s.at[s], v_r.at[s], v_devs[s])
 
-    first = 6 + n_pairs
+    first = 7 + n_pairs
 
     def tail(i):
         for s in range(len(v_devs) + 1):
@@ -814,9 +811,9 @@
         name="layer",
     )(lens, tokens, cot, g1, s1, ob, g2, s2, db, ub, qvb, wqt, wo, wu, wd)
 
-    steps = 8
+    steps = 4
     part, rpart = d // steps, rows // steps
-    opart = hw // 2
+    opart = hw
 
     def finish(down, up, rest, lo_ref, tg_ref, sm_ref, o_down, o_up, o_out, o_qkv, o_lo, o_tg,
                o_g1, o_s1, o_g2, o_s2, o_ob, o_db, o_qv, o_ub):
@@ -826,11 +823,11 @@
         o_lo[...] = lo_ref[...]
         o_tg[...] = tg_ref[...]
 
-        @pl.when(i < 2)
+        @pl.when(i == 0)
         def _():
             o_out[...] = rest[...].astype(F32)
 
-        @pl.when(i >= 2)
+        @pl.when(i > 0)
         def _():
             o_qkv[0] = rest[...].astype(F32)
 
@@ -857,8 +854,8 @@
         ),
         in_specs=[blk(0), blk(steps), blk(2 * steps), row, row, pl.BlockSpec((16, d), lambda i: (0, 0))],
         out_specs=(
-            blk(0), blk(0), pl.BlockSpec((opart, d), lambda i: (jnp.minimum(i, 1), 0)),
-            pl.BlockSpec((1, opart, d), lambda i: (jnp.maximum(i - 2, 0) // 2, jnp.maximum(i - 2, 0) % 2, 0)), row, row,
+            blk(0), blk(0), pl.BlockSpec((opart, d), lambda i: (0, 0)),
+            pl.BlockSpec((1, opart, d), lambda i: (jnp.maximum(i - 1, 0), 0, 0)), row, row,
             one, one, one, one, one, one, pl.BlockSpec((2, hw), lambda i: (0, 0)), one,
         ),
         name="finish",

time: 193 us -> 178 us (0.922)
  Pallas kernels: 191 us -> 177 us
    pallas_call x1, Pallas kernels: 182 us -> 169 us  [layer(): pl.pallas_call(functools.partial(body, n_dp), out_shape=(S((rows, d), F32...]
    pallas_call x1, Pallas kernels: 9.62 us -> 7.52 us  [layer(): pl.pallas_call(finish, grid=(steps,), out_shape=(S((ff, d), F32), S((d, f...]
where the time goes in v3:
time: 178 us; the launch traced here: 177 us
  Pallas kernels  177 us (99%)
    pallas_call x1, Pallas kernels, layer(): pl.pallas_call(functools.partial(body, n_dp), out_shape=(S((rows, d), F32...  169 us
    pallas_call x1, Pallas kernels, layer(): pl.pallas_call(finish, grid=(steps,), out_shape=(S((ff, d), F32), S((d, f...  7.52 us

profile of v3, /device:TPU:0, one launch (start us, length us, event | category | flops | bytes accessed | tf_op | source)
XLA Modules:
  0.0 177.3 jit_solution(8649748036968095755)
XLA Ops:
  0.7 169.1 %layer.1 = (f32[512,768]{1,0:T(8,128)}, f32[512,768]{1,0:T(8,128)}, bf16[2304,768]{1,0:T(8,128)(2,1)}, f32[16,768]{1,0:T(8,128)}, bf16[4,768,768]{2,1,0:T(8,128)(2,1)}) custom-call(s32[4,8]{1,0:T(4,128)} %lens.1, bf16[512,768]{1,0:T(8,128)(2,1)} %tok_in.1, bf16[512,768]{1,0:T(8,128)(2,1)} %cot_in.1, f32[768]{0:T(1024)} %g1.1, f32[768]{0:T(1024)} %s1_.1, ...), custom_call_target="tpu_custom_call" | custom-call | tf_op jit(solution)/shard_map/layer/pallas_call | solution.py:784
  169.7 7.5 %finish.1 = (f32[768,768]{1,0:T(8,128)}, f32[768,768]{1,0:T(8,128)}, f32[192,768]{1,0:T(8,128)}, f32[3,192,768]{2,1,0:T(8,128)}, f32[512,768]{1,0:T(8,128)}, /*i...) custom-call(bf16[2304,768]{1,0:T(8,128)(2,1)} %get-tuple-element.32., ...), custom_call_target="tpu_custom_call" | custom-call | tf_op jit(solution)/shard_map/finish/pallas_call | solution.py:848
